TPU v7x, 32 devices: a whole 2x2x4 slice. The times are simulated.
32 devices in a mesh: src: 4 (over y, core), dst: 8 (over z, x).
Axes of the slice: x: 2, y: 2, z: 4, core: 2. Of those that a mesh axis runs over, the one named last changes fastest.
Arguments:
- normed: bfloat16 [2, 16384], replicated, may hold values from -15 to 15
- qkv_weight: bfloat16 [16384, 18432], P(('src', 'dst')), may hold values from -0.046875 to 0.046875
- out_weight: bfloat16 [16384, 16384], P('dst', 'src'), may hold values from -0.046875 to 0.046875
- prefill_pool: bfloat16 [128, 8, 64, 256], P('src', 'dst'), may hold values from -52 to 52
- page_table: int32 [2, 96], replicated, may hold values from 0 to 127, as said below
- lengths: int32 [2], replicated, may hold values from 1985 to 6144, as said below
- selected: int32 [2, 8, 32], replicated, may hold values from 0 to 95, as said below
- handoff: int32 [1, 128], replicated, may hold values from 0 to 3, as said below
Outputs:
- attn_out: float32 [2, 16384], P(None, 'src')
- decode_pool: bfloat16 [128, 8, 64, 256], P('src', 'dst')
Inputs may be any that keep to these rules, and one draw needn't show every extreme that they name: `page_table`: within each group the pages of its 2 requests, ceil(lengths / 64) each, fill every slot of the group's pool exactly once; a request's pages lie in page order over owners (owner = slot // 32); entries past a request's last page are 0. `lengths`: each request has 32 or more pages; in each group the page counts sum to 128 and one request has exactly 96 pages. `selected`: distinct page numbers below the request's page count. `handoff`: each decoder index receives exactly 32 slots of every group and at most 9 of one owner's slots; in every group some owner hands exactly 9 slots to some decoder.
All inputs are finite; a program needn't handle non-finite values.
Results may differ from a plain program's by a relative error of at most 0.02.
The roundings to bfloat16 on the way count: a program that leaves them out, or rounds other values in their place, can miss the bound.
Values may be sent and summed in bfloat16 or wider, within the bound.
No kernel may reach another device: no remote copies, remote signals or barrier semaphores. Data moves between devices by JAX's collectives and lax.ppermute only.
A program may use at most 128 MiB of HBM per device.

v0:
```python
import jax
import jax.numpy as jnp
from jax import lax
from jax.sharding import PartitionSpec as P

QH = 128
KVH = 8


NEG_FILL = -1e30
ROPE_BASE = 500000.0


def combined_all(part, axis, combine):
    gathered = jax.tree.map(lambda a: lax.all_gather(a, axis), part)

    def take(source):
        return jax.tree.map(lambda a: lax.dynamic_index_in_dim(a, source, 0, False), gathered)

    return lax.fori_loop(
        1, lax.axis_size(axis), lambda source, state: combine(state, take(source)), take(0)
    )


def rotate(vectors, positions):
    half_dim = vectors.shape[-1] // 2
    frequency = ROPE_BASE ** (-2.0 * jnp.arange(half_dim, dtype=jnp.float32) / vectors.shape[-1])
    angles = positions[..., None] * frequency
    cosine = jnp.cos(angles)
    sine_part = jnp.sin(angles)
    first_half = vectors[..., :half_dim]
    second = vectors[..., half_dim:]
    return jnp.concatenate(
        [first_half * cosine - second * sine_part, second * cosine + first_half * sine_part],
        axis=-1,
    )


def pack_pages(local_pages, destinations, first_slot, owners, capacity):
    slot_count = destinations.shape[0]
    onehot = (destinations[:, None] == jnp.arange(owners, dtype=jnp.int32)[None, :]).astype(
        jnp.int32
    )
    slot_rank = jnp.sum((jnp.cumsum(onehot, axis=0) - onehot) * onehot, axis=1)
    position = destinations * capacity + slot_rank
    target = jnp.arange(owners * capacity, dtype=jnp.int32)
    matches = (position[None, :] == target[:, None]).astype(jnp.int32)
    is_live = jnp.sum(matches, axis=1) > 0
    picked = jnp.sum(matches * jnp.arange(slot_count, dtype=jnp.int32)[None, :], axis=1)
    packed = jnp.where(
        is_live[:, None, None],
        jnp.take(local_pages, picked, axis=0),
        jnp.zeros((), local_pages.dtype),
    )
    packed_ids = jnp.where(is_live, first_slot + picked, -1)
    return (
        packed.reshape((owners, capacity) + local_pages.shape[1:]),
        packed_ids.reshape(owners, capacity),
    )


def compact(pages_in, ids_in, slot_count):
    flat_pages = pages_in.reshape((-1,) + pages_in.shape[2:])
    flat_ids = ids_in.reshape(-1)
    is_live = (flat_ids >= 0).astype(jnp.int32)
    running = jnp.cumsum(is_live) - 1
    target = jnp.arange(slot_count, dtype=jnp.int32)
    matches = ((is_live[None, :] > 0) & (running[None, :] == target[:, None])).astype(jnp.int32)
    picked = jnp.sum(matches * jnp.arange(flat_ids.shape[0], dtype=jnp.int32)[None, :], axis=1)
    return (jnp.take(flat_pages, picked, axis=0), jnp.take(flat_ids, picked, axis=0))


def slot_facts(slot_ids, page_table, group_lengths, sel_rows, group_id, req_group, page_len):
    table_rows = lax.dynamic_slice_in_dim(page_table, group_id * req_group, req_group, 0)
    page_counts = (group_lengths + page_len - 1) // page_len
    page_index = jnp.arange(table_rows.shape[1], dtype=jnp.int32)
    is_valid = page_index[None, :] < page_counts[:, None]
    slot_hit = (is_valid[:, :, None] & (table_rows[:, :, None] == slot_ids[None, None, :])).astype(
        jnp.int32
    )
    is_live = jnp.sum(slot_hit, axis=(0, 1)) > 0
    owner_req = jnp.sum(
        slot_hit * jnp.arange(req_group, dtype=jnp.int32)[:, None, None], axis=(0, 1)
    )
    page_of_slot = jnp.sum(slot_hit * page_index[None, :, None], axis=(0, 1))
    member = (owner_req[:, None] == jnp.arange(req_group, dtype=jnp.int32)[None, :]) & is_live[
        :, None
    ]
    chosen = jnp.any(
        member[:, :, None] & (sel_rows[None, :, :] == page_of_slot[:, None, None]), axis=(1, 2)
    )
    length_of_slot = jnp.sum(member.astype(jnp.int32) * group_lengths[None, :], axis=1)
    token_pos = page_of_slot[:, None] * page_len + jnp.arange(page_len, dtype=jnp.int32)[None, :]
    keep_mask = chosen[:, None] & (token_pos < length_of_slot[:, None])
    return (member, keep_mask)


def attend(queries, pages, member, keep_mask):
    head_dim = queries.shape[2]
    scores = jnp.einsum(
        "rcd,npd->rcnp", queries, pages[:, :, :head_dim], preferred_element_type=jnp.float32
    )
    key_mask = (jnp.transpose(member)[:, :, None] & keep_mask[None, :, :])[:, None]
    reduce_axes = (2, 3)
    top_score = jnp.max(jnp.where(key_mask, scores, NEG_FILL), axis=reduce_axes, keepdims=True)
    weight = jnp.where(key_mask, jnp.exp(scores - top_score), 0.0)
    weight_sum = jnp.sum(weight, axis=reduce_axes)
    einsum_form = "rcnp,npd->rcd"
    weighted = jnp.einsum(
        einsum_form,
        weight.astype(jnp.bfloat16),
        pages[:, :, head_dim:],
        preferred_element_type=jnp.float32,
    )
    return (jnp.squeeze(top_score, axis=reduce_axes), weight_sum, weighted)


def combine(earlier, later):
    top_first, sum_first, weighted_first = earlier
    top_later, sum_later, weighted_later = later
    overall = jnp.maximum(top_first, top_later)
    factor_first = jnp.exp(top_first - overall)
    factor_later = jnp.exp(top_later - overall)
    return (
        overall,
        sum_first * factor_first + sum_later * factor_later,
        weighted_first * factor_first[..., None] + weighted_later * factor_later[..., None],
    )


def shards(normed, qkv_weight, out_weight, prefill_pool, page_table, lengths, selected, handoff):
    owners = lax.axis_size("src")
    owner_id = lax.axis_index("src")
    decoders = lax.axis_size("dst")
    decoder_id = lax.axis_index("dst")
    groups = decoders // KVH
    group_id = decoder_id // KVH
    head_id = decoder_id % KVH
    req_group = normed.shape[0] // groups
    heads_q = QH // KVH
    local_pages = prefill_pool[:, 0]
    slot_count = local_pages.shape[0]
    page_len = local_pages.shape[1]
    capacity = slot_count // owners + 1
    row_count = qkv_weight.shape[0]
    row_block = owner_id * decoders + decoder_id
    token_rows = lax.dynamic_slice_in_dim(normed, row_block * row_count, row_count, 1).reshape(
        groups, req_group, row_count
    )
    weight_heads = qkv_weight.reshape(row_count, KVH, -1)
    targets = jnp.arange(1 * lax.axis_size("dst"), dtype=jnp.int32)
    part_weight = jnp.take(weight_heads, targets % KVH, axis=1)
    part_tokens = jnp.take(token_rows, targets // KVH, axis=0)
    own_share = lax.psum_scatter(
        jnp.einsum("tir,rtc->tic", part_tokens, part_weight, preferred_element_type=jnp.float32),
        "dst",
        scatter_dimension=0,
        tiled=True,
    )
    summed = lax.psum(own_share[0], "src")
    projected = summed.reshape(req_group, heads_q + 2, -1)
    head_dim = projected.shape[2]
    group_lengths = lax.dynamic_slice_in_dim(lengths, group_id * req_group, req_group, 0)
    positions = group_lengths.astype(jnp.float32)
    queries = (rotate(projected[:, :heads_q], positions[:, None]) * head_dim ** (-0.5)).astype(
        jnp.bfloat16
    )
    key_new = rotate(projected[:, heads_q], positions)
    value_new = projected[:, heads_q + 1]
    group_selected = lax.dynamic_slice_in_dim(selected, group_id * req_group, req_group, 0)
    sel_rows = lax.dynamic_index_in_dim(group_selected, head_id, 1, keepdims=False)
    destinations = lax.dynamic_slice(handoff, (group_id, owner_id * slot_count), (1, slot_count))[0]
    packed_pages, packed_ids = pack_pages(
        local_pages, destinations, owner_id * slot_count, owners, capacity
    )
    pages_in, ids_in = (
        lax.all_to_all(packed_pages, "src", split_axis=0, concat_axis=0, tiled=True),
        lax.all_to_all(packed_ids, "src", split_axis=0, concat_axis=0, tiled=True),
    )
    decode_pages, decode_ids = compact(pages_in, ids_in, slot_count)
    member, keep_mask = slot_facts(
        decode_ids, page_table, group_lengths, sel_rows, group_id, req_group, page_len
    )
    partial_out = attend(queries, decode_pages, member, keep_mask)
    top_score, weight_sum, weighted = combined_all(partial_out, "src", combine)
    own_score = jnp.sum(queries.astype(jnp.float32) * key_new[:, None, :], axis=-1)
    newest = jnp.maximum(top_score, own_score)
    old_factor = jnp.exp(top_score - newest)
    own_weight = jnp.exp(own_score - newest)
    numerator = weighted * old_factor[..., None] + own_weight[..., None] * value_new[:, None, :]
    denominator = weight_sum * old_factor + own_weight
    attended = (numerator / denominator[..., None]).astype(jnp.bfloat16)
    every_head = lax.all_gather(attended.reshape(req_group, -1), "dst", axis=0, tiled=True)
    head_block = every_head.reshape(groups, KVH, req_group, -1)
    rows_out = out_weight.shape[0]
    out_head = decoder_id // groups
    out_part = decoder_id % groups
    mine_heads = lax.dynamic_index_in_dim(head_block, out_head, 1, keepdims=False).reshape(
        groups * req_group, -1
    )
    columns = lax.dynamic_slice_in_dim(mine_heads, out_part * rows_out, rows_out, 1)
    partial_proj = jnp.dot(columns, out_weight, preferred_element_type=jnp.float32)
    attn_out = lax.psum(partial_proj.astype(jnp.bfloat16), "dst").astype(jnp.float32)
    return (attn_out, decode_pages[:, None])


def solution(mesh):
    return jax.shard_map(
        shards,
        mesh=mesh,
        in_specs=(
            P(),
            P(("src", "dst"), None),
            P("dst", "src"),
            P("src", "dst", None, None),
            P(),
            P(),
            P(),
            P(),
        ),
        out_specs=(P(None, "src"), P("src", "dst", None, None)),
        check_vma=False,
    )
```

profile of v0, /device:TPU:0, one launch (start us, length us, event | category | flops | bytes accessed | tf_op | source)
XLA Modules:
  0.0 285.5 jit_solution(13900615619706002555)
XLA Ops:
  7.3 24.8 %copy.27 = bf16[512,18432]{0,1:T(8,128)(2,1)} copy(bf16[512,18432]{1,0:T(8,128)(2,1)} %param.11) | data formatting | bytes 37748736 | tf_op args[1]
  32.1 14.7 %fusion.43 = (bf16[512,8,1152]{0,2,1:T(8,128)(2,1)}, bf16[512,8,1152]{0,2,1:T(8,128)(2,1)}) fusion(bf16[512,8,2304]{0,2,1:T(8,128)(2,1)} %bitcast.84), kind=kLoop, calls=%fused_computation.131 | loop fusion | bytes 37748736 | tf_op jit(solution)/shard_map/jit(_take)/gather | solution.py:152
  46.8 12.7 %copy.33 = bf16[512,8,1152]{2,0,1:T(8,128)(2,1)} copy(bf16[512,8,1152]{0,2,1:T(8,128)(2,1)} %get-tuple-element.227) | data formatting | bytes 18874368
  59.5 12.6 %copy.34 = bf16[512,8,1152]{2,0,1:T(8,128)(2,1)} copy(bf16[512,8,1152]{0,2,1:T(8,128)(2,1)} %get-tuple-element.228) | data formatting | bytes 18874368
  72.1 9.1 %gather_fusion.3 = bf16[8,512,1152]{2,1,0:T(8,128)(2,1)} fusion(bf16[512,8,1152]{2,0,1:T(8,128)(2,1)} %copy.33, s32[1024]{0:T(1024)S(1)} %pad_clamp_fusion.1), kind=kCustom, calls=%fused_computation.3 | custom fusion | bytes 18874400 | tf_op jit(solution)/shard_map/jit(_take)/gather | solution.py:152
  81.1 9.0 %gather_fusion.4 = bf16[8,512,1152]{2,1,0:T(8,128)(2,1)} fusion(bf16[512,8,1152]{2,0,1:T(8,128)(2,1)} %copy.34, s32[1024]{0:T(1024)S(1)} %pad_clamp_fusion.1), kind=kCustom, calls=%fused_computation.4 | custom fusion | bytes 18874400 | tf_op jit(solution)/shard_map/jit(_take)/gather | solution.py:152
  90.1 0.7 constant_dynamic-slice_fusion.1
  90.8 8.9 %fusion.3 = f32[8,2,2304]{2,1,0:T(2,128)} fusion(bf16[512,8,1152]{2,0,1:T(8,128)(2,1)} %bitcast.86, bf16[512,8,1152]{2,0,1:T(8,128)(2,1)} %bitcast.85, pred[8]{0:T(512)(128)(4,1)S(1)} %get-tuple-element.241, pred[8]{0:T(512)(128)(4,1)S(1)} %get-tuple-element.242, bf16[2,512]{1,0:T(2,128)(2,1)S(1)} %constant_dynamic-slice_fusion.1), kind=kOutput, calls=%fused_computation.15 | convolution fusion | flops 84942848 | bytes 19023888 | tf_op jit(solution)/shard_map/tir,rtc->tic/dot_general | solution.py:155
  101.0 4.3 %all-to-all-start = ((s32[4,1,9]{2,1,0:T(1,128)}), s32[4,1,9]{2,1,0:T(1,128)S(1)}, u32[]{:S(2)}, u32[]{:S(2)}) async-start(s32[4,1,9]{2,1,0:T(1,128)} %bitcast.6), calls=%async_computation | async-start | bytes 4096 | tf_op jit(solution)/shard_map/all_to_all | solution.py:178
  106.2 0.7 constant_dynamic-slice_fusion.2
  107.5 1.5 all-to-all-done
  110.7 0.7 gather_fusion
  111.8 1.2 select_select_fusion
  113.0 3.5 %all-to-all-start.1 = ((bf16[4,9,64,256]{3,2,1,0:T(8,128)(2,1)}), bf16[4,9,64,256]{3,2,1,0:T(8,128)(2,1)S(1)}, u32[]{:S(2)}, u32[]{:S(2)}) async-start(bf16[4,9,64,256]{3,2,1,0:T(8,128)(2,1)} %select_select_fusion), calls=%async_computation.1 | async-start | bytes 2359296 | tf_op jit(solution)/shard_map/all_to_all | solution.py:177
  116.9 56.2 %all-reduce.3.cloned.1.call-done = f32[8,2,2304]{2,1,0:T(2,128)} async-done(((f32[8,2,2304]{2,1,0:T(2,128)}), f32[8,2,2304]{2,1,0:T(2,128)}) %all-reduce.3.cloned.1.call-update) | async-done | bytes 147472
  173.1 1.4 constant_dynamic-slice_fusion.4
  174.5 10.3 %psum.14 = f32[2,18,128]{2,1,0:T(8,128)S(1)} all-reduce(f32[2,18,128]{2,1,0:T(8,128)S(1)} %reshape.476), channel_id=1, replica_groups=mesh['src'=4,'dst'=8] {'src'}, use_global_device_ids=true, to_apply=%region_12.13 | all-reduce | flops 4608 | bytes 36864 | tf_op jit(solution)/shard_map/psum | solution.py:160
  187.3 1.2 fusion.8
  188.5 5.2 %all-gather.2 = f32[8,16,128]{2,1,0:T(8,128)S(1)} all-gather(f32[2,16,128]{2,1,0:T(8,128)S(1)} %convolution_bitcast_fusion), channel_id=4, replica_groups=mesh['src'=4,'dst'=8] {'src'}, dimensions={0}, use_global_device_ids=true | all-gather | bytes 81920 | tf_op jit(solution)/shard_map/all_gather | solution.py:15
  193.7 5.1 %all-gather.4 = f32[4,2,16]{2,1,0:T(2,128)S(1)} all-gather(f32[1,2,16]{2,1,0:T(2,128)S(1)} %bitcast.92), channel_id=3, replica_groups=mesh['src'=4,'dst'=8] {'src'}, dimensions={0}, use_global_device_ids=true | all-gather | bytes 640 | tf_op jit(solution)/shard_map/all_gather | solution.py:15
  198.8 5.1 %all-gather.3 = f32[4,2,16]{2,1,0:T(2,128)S(1)} all-gather(f32[1,2,16]{2,1,0:T(2,128)S(1)} %bitcast.90), channel_id=2, replica_groups=mesh['src'=4,'dst'=8] {'src'}, dimensions={0}, use_global_device_ids=true | all-gather | bytes 640 | tf_op jit(solution)/shard_map/all_gather | solution.py:15
  204.2 30.5 %all-gather.5 = bf16[8,2,2048]{2,1,0:T(2,128)(2,1)S(1)} all-gather(bf16[1,2,2048]{2,1,0:T(2,128)(2,1)S(1)} %reshape.538), channel_id=1, replica_groups=mesh['src'=4,'dst'=8] {'dst'}, dimensions={0}, use_global_device_ids=true | all-gather | bytes 73728 | tf_op jit(solution)/shard_map/all_gather | solution.py:193
  234.8 8.0 %convolution_convert_fusion = bf16[2,4096]{1,0:T(2,128)(2,1)S(1)} fusion(bf16[2048,4096]{1,0:T(8,128)(2,1)} %param.12, bf16[8,2,2048]{2,1,0:T(2,128)(2,1)S(1)} %all-gather.5, s32[]{:T(128)S(6)} %select_n.243), kind=kOutput, calls=%fused_computation.20 | convolution fusion | flops 33562624 | bytes 16801796 | tf_op jit(solution)/shard_map/dot_general | solution.py:202
  242.8 35.2 %psum.15 = bf16[2,4096]{1,0:T(2,128)(2,1)S(1)} all-reduce(bf16[2,4096]{1,0:T(2,128)(2,1)S(1)} %convolution_convert_fusion), channel_id=1, replica_groups=mesh['src'=4,'dst'=8] {'dst'}, use_global_device_ids=true, to_apply=%region_18.19 | all-reduce | flops 8192 | bytes 32768 | tf_op jit(solution)/shard_map/psum | solution.py:203
  (78 shorter events, 9.1 us)
Async XLA Ops:
  7.2 99.7 %copy-start = (bf16[32,1,64,256]{3,2,1,0:T(8,128)(2,1)S(1)}, bf16[32,1,64,256]{3,2,1,0:T(8,128)(2,1)}, u32[]{:S(2)}) copy-start(bf16[32,1,64,256]{3,2,1,0:T(8,128)(2,1)} %param.13) | copy-start | bytes 3145732
  7.2 165.9 %all-reduce.3.cloned.1.call-start = ((), (), s32[]{:S(2)}) async-start(), calls=%async_computation.2 | async-start | bytes 294912
  90.8 9.0 %copy-start.3 = (s32[1,128]{1,0:T(1,128)S(1)}, s32[1,128]{1,0:T(1,128)}, u32[]{:S(2)}) copy-start(s32[1,128]{1,0:T(1,128)} %param.17) | copy-start | bytes 1540
  90.8 14.6 %copy-start.2 = (s32[2]{0:T(128)S(1)}, s32[2]{0:T(128)}, u32[]{:S(2)}) copy-start(s32[2]{0:T(128)} %param.15) | copy-start | bytes 28
  90.8 14.7 %copy-start.4 = (u32[32]{0:T(128)S(1)}, u32[32]{0:T(128)}, u32[]{:S(2)}) copy-start(u32[32]{0:T(128)} %constant.267) | copy-start | bytes 388
  90.8 20.5 %copy-start.1 = (s32[2,96]{1,0:T(2,128)S(1)}, s32[2,96]{1,0:T(2,128)}, u32[]{:S(2)}) copy-start(s32[2,96]{1,0:T(2,128)} %param.14) | copy-start | bytes 2308
  101.0 8.0 %all-to-all-start = ((s32[4,1,9]{2,1,0:T(1,128)}), s32[4,1,9]{2,1,0:T(1,128)S(1)}, u32[]{:S(2)}, u32[]{:S(2)}) async-start(s32[4,1,9]{2,1,0:T(1,128)} %bitcast.6), calls=%async_computation | async-start | bytes 4096 | tf_op jit(solution)/shard_map/all_to_all | solution.py:178
  113.0 72.2 %all-to-all-start.1 = ((bf16[4,9,64,256]{3,2,1,0:T(8,128)(2,1)}), bf16[4,9,64,256]{3,2,1,0:T(8,128)(2,1)S(1)}, u32[]{:S(2)}, u32[]{:S(2)}) async-start(bf16[4,9,64,256]{3,2,1,0:T(8,128)(2,1)} %select_select_fusion), calls=%async_computation.1 | async-start | bytes 2359296 | tf_op jit(solution)/shard_map/all_to_all | solution.py:177
Sparse Core Ops, SparseCore 0:
  99.9 73.1 all-reduce.2
where the time goes:
time: 287 us; the launch traced here: 286 us
  blocking collectives  91.4 us (32%)
  local copies, waits for them, and re-layouts  89.9 us (31%)
  waiting for transfers between devices  57.7 us (20%)
  matrix products  18 us (6%)
  between operations  14.3 us (5%)
  starting transfers between devices  7.83 us (3%)
  other arithmetic  6.52 us (2%)
    unnamed x2, waiting for transfers between devices  56.2 us
    unnamed x16, local copies, waits for them, and re-layouts  52.2 us
    psum x1, blocking collectives, shards(): lax.psum(partial_proj.astype(jnp.bfloat16), 'dst').astype(jnp.float32)  35.2 us
    gather x3, local copies, waits for them, and re-layouts, shards(): part_weight = jnp.take(weight_heads, targets % KVH, axis=1)  32.8 us
    all_gather x1, blocking collectives, shards(): lax.all_gather(attended.reshape(req_group, -1), 'dst', axis=0, tiled=True)  30.5 us
    all_gather x3, blocking collectives, combined_all(): gathered = jax.tree.map(lambda a: lax.all_gather(a, axis), part)  15.3 us
    psum x1, blocking collectives, shards(): summed = lax.psum(own_share[0], 'src')  10.3 us
    dot_general x1, matrix products, shards(): jnp.einsum('tir,rtc->tic', part_tokens, part_weight, preferred_element_ty...  8.9 us
  transfers between devices with their start and end apart: 3, of which 2 were waited for; matrix products, arithmetic and copies ran while one was open for 3% of the time, Pallas kernels for 0%

commit v1 on v0

v1 whole, which is shorter than its diff:
```python
import functools

import jax
import jax.numpy as jnp
import numpy as np
from jax import lax
from jax.experimental import pallas as pl
from jax.experimental.pallas import tpu as pltpu
from jax.sharding import PartitionSpec as P

QH = 128
KVH = 8
GRP = QH // KVH

NEG_FILL = -1e30
ROPE_BASE = 500000.0

SMEM = pl.BlockSpec(memory_space=pltpu.SMEM)
VMEM = pl.BlockSpec(memory_space=pltpu.VMEM)
ANY = pl.BlockSpec(memory_space=pl.ANY)


def frequencies(head_dim):
    half = np.arange(head_dim // 2, dtype=np.float64)
    frequency = ROPE_BASE ** (-2.0 * half / head_dim)
    return np.concatenate([frequency, frequency]).astype(np.float32)


def pack_body(handoff, pool, packed, count, sem):
    owners = packed.shape[0]
    slots = pool.shape[0]
    group = lax.axis_index("dst") // KVH
    first = lax.axis_index("src") * slots
    for decoder in range(owners):
        count[decoder] = 0

    def send(slot, carry):
        decoder = handoff[group, first + slot]
        place = count[decoder]
        count[decoder] = place + 1
        pltpu.make_async_copy(pool.at[slot], packed.at[decoder, place], sem).start()
        return carry

    lax.fori_loop(0, slots, send, 0)
    pltpu.make_async_copy(pool, pool, sem).wait()


def pack(handoff, pool, owners, capacity):
    return pl.pallas_call(
        pack_body,
        out_shape=jax.ShapeDtypeStruct((owners, capacity) + pool.shape[1:], pool.dtype),
        in_specs=[SMEM, ANY],
        out_specs=ANY,
        scratch_shapes=[pltpu.SMEM((owners,), jnp.int32), pltpu.SemaphoreType.DMA],
        name="pack",
    )(handoff, pool)


def project_body(
    page_len, handoff, table, lengths, selected, frequency, tokens, weight,
    out, live, cosine, sine, source, limit,
):
    groups, _, rows, head_dim = out.shape
    parts = GRP + 2
    reqs = rows // parts
    slots = source.shape[0] // 2
    step = pl.program_id(0)
    me = lax.axis_index("src")
    group = lax.axis_index("dst") // KVH
    head = lax.axis_index("dst") % KVH

    result = jnp.dot(tokens[...], weight[...], preferred_element_type=jnp.float32)
    for g in range(groups):
        for part in range(parts):
            out[g, 0, part * reqs : (part + 1) * reqs, :] = result[
                g * reqs : (g + 1) * reqs, part * head_dim : (part + 1) * head_dim
            ]

    @pl.when(step == 1)
    def _():
        def clear(index, carry):
            limit[index] = 0
            return carry

        lax.fori_loop(0, reqs * slots, clear, 0)
        for r in range(reqs):
            length = lengths[group * reqs + r]

            def mark(entry, carry, r=r, length=length):
                page = selected[group * reqs + r, head, entry]
                slot = table[group * reqs + r, page]
                mine = slot // slots == me
                place = jnp.where(mine, r * slots + slot % slots, reqs * slots)
                limit[place] = length - page * page_len
                return carry

            lax.fori_loop(0, selected.shape[2], mark, 0)

    @pl.when(step == 2)
    def _():
        lane = lax.broadcasted_iota(jnp.int32, (1, 128), 1)
        per = 128 // page_len
        for r in range(reqs):
            for chunk in range(slots // per):
                bound = jnp.full((1, 128), limit[r * slots + chunk * per], jnp.int32)
                for k in range(1, per):
                    bound = jnp.where(
                        lane >= k * page_len, limit[r * slots + chunk * per + k], bound
                    )
                live[r : r + 1, chunk * 128 : (chunk + 1) * 128] = jnp.where(
                    lane % page_len < bound, 1.0, 0.0
                )

    @pl.when(step == 3)
    def _():
        lane = lax.broadcasted_iota(jnp.int32, (1, head_dim), 1)
        for r in range(reqs):
            position = lengths[group * reqs + r].astype(jnp.float32)
            angle = frequency[...] * position
            cosine[r : r + 1, :] = jnp.cos(angle)
            sine[r : r + 1, :] = jnp.where(lane < head_dim // 2, -jnp.sin(angle), jnp.sin(angle))

    @pl.when(step == 4)
    def _():
        owners = handoff.shape[1] // slots
        capacity = slots // owners + 1

        def owner_pages(owner, filled):
            def look(slot, state):
                filled, taken = state
                hit = handoff[group, owner * slots + slot] == me
                source[jnp.where(hit, filled, slots)] = owner * capacity + taken
                one = hit.astype(jnp.int32)
                return filled + one, taken + one

            return lax.fori_loop(0, slots, look, (filled, 0))[0]

        lax.fori_loop(0, owners, owner_pages, 0)


def project(handoff, table, lengths, selected, tokens, weight, groups, slots, page_len):
    reqs_all, rows = tokens.shape
    reqs = reqs_all // groups
    width = weight.shape[1] // KVH
    head_dim = width // (GRP + 2)
    frequency = jnp.asarray(frequencies(head_dim))[None]

    def fixed(shape):
        return pl.BlockSpec(shape, lambda i: (0,) * len(shape))

    return pl.pallas_call(
        functools.partial(project_body, page_len),
        grid=(KVH,),
        in_specs=[
            SMEM, SMEM, SMEM, SMEM,
            fixed((1, head_dim)),
            fixed((reqs_all, rows)),
            pl.BlockSpec((rows, width), lambda i: (0, i)),
        ],
        out_specs=[
            pl.BlockSpec((groups, 1, (GRP + 2) * reqs, head_dim), lambda i: (0, i, 0, 0)),
            fixed((reqs, slots * page_len)),
            fixed((reqs, head_dim)),
            fixed((reqs, head_dim)),
            SMEM,
        ],
        out_shape=[
            jax.ShapeDtypeStruct((groups, KVH, (GRP + 2) * reqs, head_dim), jnp.float32),
            jax.ShapeDtypeStruct((reqs, slots * page_len), jnp.float32),
            jax.ShapeDtypeStruct((reqs, head_dim), jnp.float32),
            jax.ShapeDtypeStruct((reqs, head_dim), jnp.float32),
            jax.ShapeDtypeStruct((2 * slots,), jnp.int32),
        ],
        scratch_shapes=[pltpu.SMEM((reqs * slots + 1,), jnp.int32)],
        compiler_params=pltpu.CompilerParams(vmem_limit_bytes=24 * 1024 * 1024),
        name="project",
    )(handoff, table, lengths, selected, frequency, tokens, weight)


def attend_body(parts, pool, live, cosine, sine, out):
    total = parts[0]
    for source in range(1, parts.shape[0]):
        total = total + parts[source]
    head_dim = total.shape[1]
    reqs = live.shape[0]
    rows = GRP * reqs

    def per_row(values, count):
        row = lax.broadcasted_iota(jnp.int32, (count, 1), 0) % reqs
        wide = jnp.broadcast_to(values[0:1], (count, values.shape[1]))
        for r in range(1, reqs):
            wide = jnp.where(row == r, values[r : r + 1], wide)
        return wide

    turned = total[: rows + reqs]
    turned = turned * per_row(cosine[...], rows + reqs) + pltpu.roll(
        turned, head_dim // 2, 1
    ) * per_row(sine[...], rows + reqs)
    queries = (turned[:rows] * head_dim ** (-0.5)).astype(jnp.bfloat16)
    key_new = per_row(turned[rows:], rows)
    value_new = per_row(total[rows + reqs :], rows)

    pages = pool[...].reshape(-1, 2 * head_dim)
    scores = lax.dot_general(
        queries, pages[:, :head_dim], (((1,), (1,)), ((), ())),
        preferred_element_type=jnp.float32,
    )
    mask = per_row(live[...], rows) > 0.5
    own = jnp.sum(queries.astype(jnp.float32) * key_new, axis=1, keepdims=True)
    first = lax.axis_index("src") == 0
    own = jnp.where(first, own, NEG_FILL)
    top = jnp.maximum(jnp.max(jnp.where(mask, scores, NEG_FILL), axis=1, keepdims=True), own)
    weight = jnp.where(mask, jnp.exp(scores - top), 0.0)
    own_weight = jnp.where(first, jnp.exp(own - top), 0.0)
    total_weight = jnp.sum(weight, axis=1, keepdims=True) + own_weight
    weighted = (
        jnp.dot(
            weight.astype(jnp.bfloat16), pages[:, head_dim:], preferred_element_type=jnp.float32
        )
        + own_weight * value_new
    )
    out[:, :head_dim] = weighted
    lane = lax.broadcasted_iota(jnp.int32, (rows, head_dim), 1)
    out[:, head_dim:] = jnp.where(lane < head_dim // 2, top, total_weight)


def attend(parts, pool, live, cosine, sine):
    reqs = live.shape[0]
    return pl.pallas_call(
        attend_body,
        out_shape=jax.ShapeDtypeStruct((GRP * reqs, pool.shape[2]), jnp.float32),
        in_specs=[VMEM] * 5,
        out_specs=VMEM,
        compiler_params=pltpu.CompilerParams(vmem_limit_bytes=16 * 1024 * 1024),
        name="attend",
    )(parts, pool, live, cosine, sine)


def merge(parts):
    head_dim = parts.shape[-1] // 2
    half = head_dim + head_dim // 2
    tops = [parts[s, :, head_dim : head_dim + 1] for s in range(parts.shape[0])]
    overall = functools.reduce(jnp.maximum, tops)
    numerator = denominator = 0.0
    for s, top in enumerate(tops):
        factor = jnp.exp(top - overall)
        numerator = numerator + parts[s, :, :head_dim] * factor
        denominator = denominator + parts[s, :, half : half + 1] * factor
    return numerator / denominator


def output_body(merged, source, heads, pages, weight, out, pool, tokens, sem):
    step = pl.program_id(0)
    slots = pool.shape[0]
    copies = out.shape[0]
    depth = weight.shape[0]

    @pl.when(step == 0)
    def _():
        def place(slot, carry):
            pltpu.make_async_copy(pages.at[source[slot]], pool.at[slot], sem).start()
            return carry

        lax.fori_loop(0, slots, place, 0)
        if merged:
            reqs = tokens.shape[0]
            attended = merge(heads)
            head_dim = attended.shape[1]
            for c in range(GRP):
                tokens[:, c * head_dim : (c + 1) * head_dim] = attended[c * reqs : (c + 1) * reqs]
        else:
            tokens[...] = heads[...].astype(jnp.float32)

    result = jnp.dot(
        tokens[...].astype(jnp.bfloat16), weight[...], preferred_element_type=jnp.float32
    ).astype(out.dtype)
    for copy in range(copies):
        out[copy] = result

    @pl.when(step == pl.num_programs(0) - 1)
    def _():
        pltpu.make_async_copy(pool, pool, sem).wait()


def output(source, heads, pages, weight, reqs, copies, slots, merged):
    depth, width = weight.shape
    tile = width // 8 if width % 1024 == 0 else width
    return pl.pallas_call(
        functools.partial(output_body, merged),
        grid=(width // tile,),
        in_specs=[
            SMEM,
            pl.BlockSpec(heads.shape, lambda i: (0,) * heads.ndim),
            ANY,
            pl.BlockSpec((depth, tile), lambda i: (0, i)),
        ],
        out_specs=[pl.BlockSpec((copies, reqs, tile), lambda i: (0, 0, i)), ANY],
        out_shape=[
            jax.ShapeDtypeStruct((copies, reqs, width), jnp.bfloat16),
            jax.ShapeDtypeStruct((slots,) + pages.shape[1:], pages.dtype),
        ],
        scratch_shapes=[pltpu.VMEM((reqs, depth), jnp.float32), pltpu.SemaphoreType.DMA],
        compiler_params=pltpu.CompilerParams(vmem_limit_bytes=24 * 1024 * 1024),
        name="output",
    )(source, heads, pages, weight)


def shards(normed, qkv_weight, out_weight, prefill_pool, page_table, lengths, selected, handoff):
    owners = lax.axis_size("src")
    decoders = lax.axis_size("dst")
    decoder_id = lax.axis_index("dst")
    groups = decoders // KVH
    reqs = normed.shape[0]
    req_group = reqs // groups
    pool = prefill_pool.reshape(prefill_pool.shape[0], *prefill_pool.shape[2:])
    slots, page_len = pool.shape[:2]
    capacity = slots // owners + 1

    packed = pack(handoff, pool, owners, capacity)
    arrived = lax.all_to_all(packed, "src", split_axis=0, concat_axis=0, tiled=True)

    rows = qkv_weight.shape[0]
    row_block = lax.axis_index("src") * decoders + decoder_id
    tokens = lax.dynamic_slice_in_dim(normed, row_block * rows, rows, 1)
    partial, live, cosine, sine, source = project(
        handoff, page_table, lengths, selected, tokens, qkv_weight, groups, slots, page_len
    )
    shares = lax.all_to_all(
        partial.reshape((decoders,) + partial.shape[2:]), "dst",
        split_axis=0, concat_axis=0, tiled=True,
    )
    projected = lax.all_gather(jnp.sum(shares, axis=0), "src")
    mine = attend(projected, pool, live, cosine, sine)
    heads = lax.all_gather(mine, "src")
    merged = groups == 1
    if not merged:
        attended = merge(heads).astype(jnp.bfloat16)
        head_dim = attended.shape[1]
        flat = attended.reshape(GRP, req_group, head_dim).transpose(1, 0, 2)
        every = lax.all_gather(flat.reshape(req_group, -1), "dst", axis=0, tiled=True)
        every = every.reshape(groups, KVH, req_group, -1)
        block = lax.dynamic_index_in_dim(every, decoder_id // groups, 1, keepdims=False)
        depth = out_weight.shape[0]
        heads = lax.dynamic_slice_in_dim(
            block.reshape(reqs, -1), (decoder_id % groups) * depth, depth, 1
        )
    outgoing, decode_pool = output(
        source, heads, arrived.reshape((-1,) + pool.shape[1:]), out_weight,
        reqs, decoders, slots, merged,
    )
    incoming = lax.all_to_all(outgoing, "dst", split_axis=0, concat_axis=0, tiled=True)
    attn_out = jnp.sum(incoming.astype(jnp.float32), axis=0)
    return attn_out, decode_pool[:, None]


def solution(mesh):
    return jax.shard_map(
        shards,
        mesh=mesh,
        in_specs=(
            P(),
            P(("src", "dst"), None),
            P("dst", "src"),
            P("src", "dst", None, None),
            P(),
            P(),
            P(),
            P(),
        ),
        out_specs=(P(None, "src"), P("src", "dst", None, None)),
        check_vma=False,
    )
```

time: 287 us -> 114 us (0.40)
  local copies, waits for them, and re-layouts: 89.9 us -> 16.3 us
  waiting for transfers between devices: 57.7 us -> 0.01 us
  blocking collectives: 91.4 us -> 35.7 us
  Pallas kernels: 0 us -> 48.7 us
  matrix products: 18 us -> 0 us
  between operations: 14.3 us -> 0.7 us
  other arithmetic: 6.52 us -> 0.74 us
  starting transfers between devices: 7.83 us -> 10.8 us
    unnamed x2 -> x0, waiting for transfers between devices: 56.2 us -> none
    pallas_call x0 -> x4, Pallas kernels: none -> 48.7 us  [the longest x1 33.6 us: pack(): pl.pallas_call(pack_body, out_shape=jax.ShapeDtypeStruct((owners, capacit...]
    psum x2 -> x0, blocking collectives: 45.5 us -> none  [the longest x1 35.2 us: shards(): lax.psum(partial_proj.astype(jnp.bfloat16), 'dst').astype(jnp.float32)]
    unnamed x16 -> x18, local copies, waits for them, and re-layouts: 52.2 us -> 16.3 us
    gather x6 -> x0, local copies, waits for them, and re-layouts: 34.7 us -> none  [the longest x3 32.8 us: shards(): part_weight = jnp.take(weight_heads, targets % KVH, axis=1)]
    all_gather x4 -> x2, blocking collectives: 45.9 us -> 22.5 us  [the longest x1 17 us: shards(): projected = lax.all_gather(jnp.sum(shares, axis=0), 'src')]
    dot_general x4 -> x0, matrix products: 18 us -> none  [the longest x1 8.9 us: shards(): jnp.einsum('tir,rtc->tic', part_tokens, part_weight, preferred_element_ty...]
    all_to_all x0 -> x1, blocking collectives: none -> 13.3 us  [shards(): lax.all_to_all(outgoing, 'dst', split_axis=0, concat_axis=0, tiled=True)]
  transfers between devices with their start and end apart: 3 -> 2, of which waited for: 2 -> 0; matrix products, arithmetic and copies ran while one was open for 3% -> 0% of each run, Pallas kernels for 0% -> 30%
where the time goes in v1:
time: 114 us; the launch traced here: 113 us
  Pallas kernels  48.7 us (43%)
  blocking collectives  35.7 us (31%)
  local copies, waits for them, and re-layouts  16.3 us (14%)
  starting transfers between devices  10.8 us (9%)
    pallas_call x1, Pallas kernels, pack(): pl.pallas_call(pack_body, out_shape=jax.ShapeDtypeStruct((owners, capacit...  33.6 us
    all_gather x1, blocking collectives, shards(): projected = lax.all_gather(jnp.sum(shares, axis=0), 'src')  17 us
    unnamed x18, local copies, waits for them, and re-layouts  16.3 us
    all_to_all x1, blocking collectives, shards(): lax.all_to_all(outgoing, 'dst', split_axis=0, concat_axis=0, tiled=True)  13.3 us
    pallas_call x1, Pallas kernels, project(): pl.pallas_call(functools.partial(project_body, page_len), grid=(KVH,), in...  9.13 us
    all_to_all x1, starting transfers between devices, shards(): lax.all_to_all(partial.reshape((decoders,) + partial.shape[2:]), 'dst', s...  7.29 us
    all_gather x1, blocking collectives, shards(): heads = lax.all_gather(mine, 'src')  5.41 us
    pallas_call x1, Pallas kernels, output(): pl.pallas_call(functools.partial(output_body, merged), grid=(width // til...  5.41 us
  transfers between devices with their start and end apart: 2, of which 0 were waited for; matrix products, arithmetic and copies ran while one was open for 0% of the time, Pallas kernels for 30%

profile of v1, /device:TPU:0, one launch (start us, length us, event | category | flops | bytes accessed | tf_op | source)
XLA Modules:
  0.0 113.1 jit_solution(10565487236397958310)
XLA Ops:
  0.6 0.0 copy-start
  0.7 0.8 copy-done
  1.5 0.0 copy-start.1
  1.5 6.4 %copy-done.1 = bf16[512,18432]{1,0:T(8,128)(2,1)S(1)} copy-done((bf16[512,18432]{1,0:T(8,128)(2,1)S(1)}, bf16[512,18432]{1,0:T(8,128)(2,1)}, u32[]{:S(2)}) %copy-start.1) | copy-done | bytes 18874392
  7.8 0.0 copy-start.4
  7.8 0.7 copy-done.4
  8.5 0.7 copy-done.5
  9.2 0.7 copy-done.6
  9.9 0.7 copy-done.7
  10.5 0.7 copy-done.8
  11.2 9.1 %project.1 = (f32[1,8,36,128]{3,2,1,0:T(8,128)}, f32[2,2048]{1,0:T(2,128)S(1)}, f32[2,128]{1,0:T(2,128)S(1)}, f32[2,128]{1,0:T(2,128)S(1)}, s32[64]{0:T(128)S(1)}) custom-call(s32[1,128]{1,0:T(1,128)S(1)} %copy-done.5, s32[2,96]{1,0:T(2,128)S(1)} %copy-done.6, s32[2]{0:T(128)S(1)} %copy-done.7, s32[2,8,32]{2,1,0:T(8,128)S(1)} %copy-done.4, ...), custom_call_target="tpu_custom_call" | custom-call | tf_op jit(solution)/shard_map/project/pallas_call | solution.py:151
  20.3 7.3 %all-to-all-start = ((f32[8,36,128]{2,1,0:T(8,128)}), f32[8,36,128]{2,1,0:T(8,128)S(1)}, u32[]{:S(2)}, u32[]{:S(2)}) async-start(f32[8,36,128]{2,1,0:T(8,128)} %bitcast), calls=%async_computation | async-start | bytes 327680 | tf_op jit(solution)/shard_map/all_to_all | solution.py:328
  27.6 33.6 %pack.1 = bf16[4,9,64,256]{3,2,1,0:T(8,128)(2,1)} custom-call(s32[1,128]{1,0:T(1,128)} %handoff.3, bf16[32,64,256]{2,1,0:T(8,128)(2,1)} %bitcast.9), custom_call_target="tpu_custom_call" | custom-call | tf_op jit(solution)/shard_map/pack/pallas_call | solution.py:49
  61.2 0.0 all-to-all-done
  61.2 3.5 %all-to-all-start.1 = ((bf16[4,9,64,256]{3,2,1,0:T(8,128)(2,1)}), bf16[4,9,64,256]{3,2,1,0:T(8,128)(2,1)S(1)}, u32[]{:S(2)}, u32[]{:S(2)}) async-start(bf16[4,9,64,256]{3,2,1,0:T(8,128)(2,1)} %pack.1), calls=%async_computation.1 | async-start | bytes 2359296 | tf_op jit(solution)/shard_map/all_to_all | solution.py:320
  64.8 17.0 %all-gather.2.parts = f32[4,36,128]{2,1,0:T(8,128)S(1)} all-gather(f32[1,36,128]{2,1,0:T(8,128)S(1)} %bitcast.12), channel_id=2, replica_groups=mesh['src'=4,'dst'=8] {'src'}, dimensions={0}, use_global_device_ids=true | all-gather | bytes 92160 | tf_op jit(solution)/shard_map/all_gather | solution.py:332
  81.8 0.0 copy-done.3
  81.8 0.6 attend.1
  82.4 5.4 %all-gather.1 = f32[128,256]{1,0:T(8,128)S(1)} all-gather(f32[32,256]{1,0:T(8,128)S(1)} %attend.1), channel_id=3, replica_groups=mesh['src'=4,'dst'=8] {'src'}, dimensions={0}, use_global_device_ids=true | all-gather | bytes 163840 | tf_op jit(solution)/shard_map/all_gather | solution.py:334
  87.8 0.0 all-to-all-done.1
  87.9 5.8 %copy-done.2 = bf16[2048,4096]{1,0:T(8,128)(2,1)S(1)} copy-done((bf16[2048,4096]{1,0:T(8,128)(2,1)S(1)}, bf16[2048,4096]{1,0:T(8,128)(2,1)}, u32[]{:S(2)}) %copy-start.2) | copy-done | bytes 16777240
  93.6 5.4 %output.1 = (bf16[8,2,4096]{2,1,0:T(2,128)(2,1)S(1)}, bf16[32,64,256]{2,1,0:T(8,128)(2,1)}) custom-call(s32[64]{0:T(128)S(1)} %get-tuple-element.9.source, f32[4,32,256]{2,1,0:T(8,128)S(1)} %bitcast.11, bf16[36,64,256]{2,1,0:T(8,128)(2,1)S(1)} %bitcast.8, bf16[2048,4096]{1,0:T(8,128)(2,1)S(1)} %copy-done.2), custom_call_target="tpu_custom_call" | custom-call | tf_op jit(solution)/shard_map/output/pallas_call | solution.py:288
  99.0 13.3 %all_to_all.15 = bf16[8,2,4096]{2,1,0:T(2,128)(2,1)S(1)} all-to-all(bf16[8,2,4096]{2,1,0:T(2,128)(2,1)S(1)} %get-tuple-element.14), channel_id=1, replica_groups=mesh['src'=4,'dst'=8] {'dst'}, dimensions={0} | all-to-all | bytes 262144 | tf_op jit(solution)/shard_map/all_to_all | solution.py:351
  112.3 0.7 convert_reduce_fusion
  (8 shorter events, 0.0 us)
Async XLA Ops:
  0.6 0.8 copy-start
  1.5 6.4 %copy-start.1 = (bf16[512,18432]{1,0:T(8,128)(2,1)S(1)}, bf16[512,18432]{1,0:T(8,128)(2,1)}, u32[]{:S(2)}) copy-start(bf16[512,18432]{1,0:T(8,128)(2,1)} %weight.2) | copy-start | bytes 56623108
  7.8 0.7 copy-start.4
  8.5 0.7 copy-start.5
  9.2 0.7 copy-start.6
  9.9 0.7 copy-start.7
  10.5 0.7 copy-start.8
  11.2 70.6 %copy-start.3 = (bf16[32,1,64,256]{3,2,1,0:T(8,128)(2,1)S(1)}, bf16[32,1,64,256]{3,2,1,0:T(8,128)(2,1)}, u32[]{:S(2)}) copy-start(bf16[32,1,64,256]{3,2,1,0:T(8,128)(2,1)} %param.12) | copy-start | bytes 3145732
  20.3 40.9 %all-to-all-start = ((f32[8,36,128]{2,1,0:T(8,128)}), f32[8,36,128]{2,1,0:T(8,128)S(1)}, u32[]{:S(2)}, u32[]{:S(2)}) async-start(f32[8,36,128]{2,1,0:T(8,128)} %bitcast), calls=%async_computation | async-start | bytes 327680 | tf_op jit(solution)/shard_map/all_to_all | solution.py:328
  61.2 26.6 %all-to-all-start.1 = ((bf16[4,9,64,256]{3,2,1,0:T(8,128)(2,1)}), bf16[4,9,64,256]{3,2,1,0:T(8,128)(2,1)S(1)}, u32[]{:S(2)}, u32[]{:S(2)}) async-start(bf16[4,9,64,256]{3,2,1,0:T(8,128)(2,1)} %pack.1), calls=%async_computation.1 | async-start | bytes 2359296 | tf_op jit(solution)/shard_map/all_to_all | solution.py:320
  87.8 5.8 %copy-start.2 = (bf16[2048,4096]{1,0:T(8,128)(2,1)S(1)}, bf16[2048,4096]{1,0:T(8,128)(2,1)}, u32[]{:S(2)}) copy-start(bf16[2048,4096]{1,0:T(8,128)(2,1)} %weight.3) | copy-start | bytes 50331652

commit v2 on v1

v2 whole, which is shorter than its diff:
```python
import functools

import jax
import jax.numpy as jnp
import numpy as np
from jax import lax
from jax.experimental import pallas as pl
from jax.experimental.pallas import tpu as pltpu
from jax.sharding import PartitionSpec as P


QH = 128
KVH = 8
GRP = QH // KVH


NEG_FILL = -1e30
ROPE_BASE = 500000.0

SMEM = pl.BlockSpec(memory_space=pltpu.SMEM)
VMEM = pl.BlockSpec(memory_space=pltpu.VMEM)
ANY = pl.BlockSpec(memory_space=pl.ANY)


def near(array):
    return pltpu.with_memory_space_constraint(array, pltpu.HBM)


def frequencies(head_dim):
    half = np.arange(head_dim // 2, dtype=np.float64)
    frequency = ROPE_BASE ** (-2.0 * half / head_dim)
    return np.concatenate([frequency, frequency]).astype(np.float32)


def pack_body(handoff, pool, *rest):
    packed, (count, sem) = rest[:-2], rest[-2:]
    owners = len(packed) + 1
    slots = pool.shape[0]
    group = lax.axis_index("dst") // KVH
    me = lax.axis_index("src")
    for offset in range(owners):
        count[offset] = 0

    def send(slot, carry):
        offset = handoff[group, me * slots + slot] ^ me
        place = count[offset]
        count[offset] = place + 1
        for other in range(1, owners):

            @pl.when(offset == other)
            def _(other=other):
                pltpu.make_async_copy(pool.at[slot], packed[other - 1].at[place], sem).start()

        return carry

    lax.fori_loop(0, slots, send, 0)

    def settle(index, carry):
        pltpu.make_async_copy(pool.at[0], packed[0].at[0], sem).wait()
        return carry

    lax.fori_loop(0, slots - count[0], settle, 0)


def pack(handoff, pool, owners, capacity):
    one = pltpu.VMEM((capacity,) + pool.shape[1:], pool.dtype)
    return pl.pallas_call(
        pack_body,
        out_shape=[one] * (owners - 1),
        in_specs=[SMEM, ANY],
        out_specs=[VMEM] * (owners - 1),
        scratch_shapes=[pltpu.SMEM((owners,), jnp.int32), pltpu.SemaphoreType.DMA],
        compiler_params=pltpu.CompilerParams(vmem_limit_bytes=4 * 1024 * 1024),
        cost_estimate=pl.CostEstimate(flops=10**10, bytes_accessed=2**25, transcendentals=0),
        name="pack",
    )(near(handoff), near(pool))


def project_body(tokens, weight, _after, out):
    groups, heads, rows, head_dim = out.shape
    parts = GRP + 2
    reqs = rows // parts
    depth = weight.shape[0]
    if tokens.shape[1] != depth:
        block = lax.axis_index("src") * lax.axis_size("dst") + lax.axis_index("dst")
        values = tokens[:, pl.ds(pl.multiple_of(block * depth, depth), depth)]
    else:
        values = tokens[...]
    width = parts * head_dim
    for head in range(heads):
        result = jnp.dot(
            values, weight[:, head * width : (head + 1) * width],
            preferred_element_type=jnp.float32,
        )
        for g in range(groups):
            for part in range(parts):
                out[g, head, part * reqs : (part + 1) * reqs, :] = result[
                    g * reqs : (g + 1) * reqs, part * head_dim : (part + 1) * head_dim
                ]


def project(tokens, weight, groups, after):
    reqs = tokens.shape[0] // groups
    parts = GRP + 2
    head_dim = weight.shape[1] // (KVH * parts)
    return pl.pallas_call(
        project_body,
        in_specs=[VMEM, VMEM, ANY],
        out_specs=VMEM,
        out_shape=pltpu.VMEM((groups, KVH, parts * reqs, head_dim), jnp.float32),
        compiler_params=pltpu.CompilerParams(vmem_limit_bytes=24 * 1024 * 1024),
        name="project",
    )(tokens, weight, after)


def plan_body(
    page_len, slots, handoff, table, lengths, selected, frequency, live, cosine, sine, source, limit
):
    reqs, head_dim = cosine.shape
    me = lax.axis_index("src")
    group = lax.axis_index("dst") // KVH
    head = lax.axis_index("dst") % KVH

    def clear(index, carry):
        limit[index] = 0
        return carry

    lax.fori_loop(0, reqs * slots, clear, 0, unroll=16)
    for r in range(reqs):
        length = lengths[group * reqs + r]

        def mark(entry, carry, r=r, length=length):
            page = selected[group * reqs + r, head, entry]
            slot = table[group * reqs + r, page]
            local = slot - me * slots
            mine = (local >= 0) & (local < slots)
            place = jnp.where(mine, r * slots + local, reqs * slots)
            limit[place] = length - page * page_len
            return carry

        lax.fori_loop(0, selected.shape[2], mark, 0, unroll=8)

    lane = lax.broadcasted_iota(jnp.int32, (1, 128), 1)
    per = 128 // page_len
    for r in range(reqs):
        for chunk in range(slots // per):
            bound = jnp.full((1, 128), limit[r * slots + chunk * per], jnp.int32)
            for k in range(1, per):
                bound = jnp.where(lane >= k * page_len, limit[r * slots + chunk * per + k], bound)
            live[r : r + 1, chunk * 128 : (chunk + 1) * 128] = jnp.where(
                lane % page_len < bound, 1.0, 0.0
            )

    row = lax.broadcasted_iota(jnp.int32, (reqs, head_dim), 0)
    place = lax.broadcasted_iota(jnp.int32, (reqs, head_dim), 1)
    position = jnp.zeros((reqs, head_dim), jnp.float32)
    for r in range(reqs):
        position = jnp.where(row == r, lengths[group * reqs + r].astype(jnp.float32), position)
    angle = frequency[...] * position
    cosine[...] = jnp.cos(angle)
    turn = jnp.sin(angle)
    sine[...] = jnp.where(place < head_dim // 2, -turn, turn)

    owners = handoff.shape[1] // slots

    def owner_pages(owner, filled):
        own = owner == me
        source[owners + (owner ^ me)] = filled

        def look(slot, taken):
            hit = handoff[group, owner * slots + slot] == me
            source[2 * owners + jnp.where(hit & own, taken, slots)] = slot
            return taken + hit.astype(jnp.int32)

        taken = lax.fori_loop(0, slots, look, 0, unroll=8)
        source[owner ^ me] = taken
        return filled + taken

    lax.fori_loop(0, owners, owner_pages, 0)


def plan(handoff, table, lengths, selected, head_dim, reqs, slots, page_len):
    owners = handoff.shape[1] // slots
    frequency = jnp.asarray(frequencies(head_dim))[None]
    return pl.pallas_call(
        functools.partial(plan_body, page_len, slots),
        in_specs=[SMEM] * 4 + [VMEM],
        out_specs=[VMEM] * 3 + [SMEM],
        out_shape=[
            jax.ShapeDtypeStruct((reqs, slots * page_len), jnp.float32),
            jax.ShapeDtypeStruct((reqs, head_dim), jnp.float32),
            jax.ShapeDtypeStruct((reqs, head_dim), jnp.float32),
            jax.ShapeDtypeStruct((2 * owners + slots + 1,), jnp.int32),
        ],
        scratch_shapes=[pltpu.SMEM((reqs * slots + 1,), jnp.int32)],
        compiler_params=pltpu.CompilerParams(vmem_limit_bytes=2 * 1024 * 1024),
        name="plan",
    )(near(handoff), near(table), near(lengths), near(selected), near(frequency))


def attend_body(parts, pool, live, cosine, sine, out):
    total = parts[0]
    for source in range(1, parts.shape[0]):
        total = total + parts[source]
    head_dim = total.shape[1]
    reqs = live.shape[0]
    rows = GRP * reqs

    def per_row(values, count):
        row = lax.broadcasted_iota(jnp.int32, (count, 1), 0) % reqs
        wide = jnp.broadcast_to(values[0:1], (count, values.shape[1]))
        for r in range(1, reqs):
            wide = jnp.where(row == r, values[r : r + 1], wide)
        return wide

    turned = total[: rows + reqs]
    turned = turned * per_row(cosine[...], rows + reqs) + pltpu.roll(
        turned, head_dim // 2, 1
    ) * per_row(sine[...], rows + reqs)
    queries = (turned[:rows] * head_dim ** (-0.5)).astype(jnp.bfloat16)
    key_new = per_row(turned[rows:], rows)
    value_new = per_row(total[rows + reqs :], rows)

    pages = pool[...].reshape(-1, 2 * head_dim)
    scores = lax.dot_general(
        queries, pages[:, :head_dim], (((1,), (1,)), ((), ())),
        preferred_element_type=jnp.float32,
    )
    mask = per_row(live[...], rows) > 0.5
    own = jnp.sum(queries.astype(jnp.float32) * key_new, axis=1, keepdims=True)
    first = lax.axis_index("src") == 0
    own = jnp.where(first, own, NEG_FILL)
    top = jnp.maximum(jnp.max(jnp.where(mask, scores, NEG_FILL), axis=1, keepdims=True), own)
    weight = jnp.where(mask, jnp.exp(scores - top), 0.0)
    own_weight = jnp.where(first, jnp.exp(own - top), 0.0)
    total_weight = jnp.sum(weight, axis=1, keepdims=True) + own_weight
    weighted = (
        jnp.dot(
            weight.astype(jnp.bfloat16), pages[:, head_dim:], preferred_element_type=jnp.float32
        )
        + own_weight * value_new
    )
    out[:, :head_dim] = weighted
    lane = lax.broadcasted_iota(jnp.int32, (rows, head_dim), 1)
    out[:, head_dim:] = jnp.where(lane < head_dim // 2, top, total_weight)


def attend(parts, pool, live, cosine, sine):
    reqs = live.shape[0]
    return pl.pallas_call(
        attend_body,
        out_shape=jax.ShapeDtypeStruct((GRP * reqs, pool.shape[2]), jnp.float32),
        in_specs=[VMEM] * 5,
        out_specs=VMEM,
        compiler_params=pltpu.CompilerParams(vmem_limit_bytes=16 * 1024 * 1024),
        cost_estimate=pl.CostEstimate(flops=10**12, bytes_accessed=2**26, transcendentals=0),
        name="attend",
    )(parts, pool, live, cosine, sine)


def merge(parts):
    head_dim = parts.shape[-1] // 2
    half = head_dim + head_dim // 2
    tops = [parts[s, :, head_dim : head_dim + 1] for s in range(parts.shape[0])]
    overall = functools.reduce(jnp.maximum, tops)
    numerator = denominator = 0.0
    for s, top in enumerate(tops):
        factor = jnp.exp(top - overall)
        numerator = numerator + parts[s, :, :head_dim] * factor
        denominator = denominator + parts[s, :, half : half + 1] * factor
    return numerator / denominator


def output_body(merged, source, heads, weight, kept, *rest):
    pages, (out, pool, tokens, stage, sem) = rest[:-5], rest[-5:]
    copies = out.shape[0]
    owners = len(pages) + 1

    def keep(index, carry):
        slot = source[2 * owners + index]
        pltpu.make_async_copy(kept.at[slot], stage.at[source[owners] + index], sem).start()
        return carry

    lax.fori_loop(0, source[0], keep, 0)
    for other in range(1, owners):

        def place(index, carry, other=other):
            target = stage.at[source[owners + other] + index]
            pltpu.make_async_copy(pages[other - 1].at[index], target, sem).start()
            return carry

        lax.fori_loop(0, source[other], place, 0)

    if merged:
        reqs = tokens.shape[0]
        attended = merge(heads)
        head_dim = attended.shape[1]
        for c in range(GRP):
            tokens[:, c * head_dim : (c + 1) * head_dim] = attended[c * reqs : (c + 1) * reqs]
        values = tokens[...].astype(jnp.bfloat16)
    else:
        values = heads[...]

    width = weight.shape[1]
    tile = width // 8 if width % 1024 == 0 else width
    ordered = pltpu.make_async_copy(stage, pool, sem)
    for start in range(0, width, tile):
        if start == width // tile // 2 * tile:
            pltpu.make_async_copy(kept, stage, sem).wait()
            ordered.start()
        result = jnp.dot(
            values, weight[:, start : start + tile], preferred_element_type=jnp.float32
        ).astype(out.dtype)
        for copy in range(copies):
            out[copy, :, start : start + tile] = result

    ordered.wait()


def output(source, heads, weight, kept, pages, reqs, copies, merged):
    depth, width = weight.shape
    return pl.pallas_call(
        functools.partial(output_body, merged),
        in_specs=[SMEM, VMEM, VMEM, ANY] + [ANY] * len(pages),
        out_specs=[VMEM, ANY],
        out_shape=[
            jax.ShapeDtypeStruct((copies, reqs, width), jnp.bfloat16),
            jax.ShapeDtypeStruct(kept.shape, kept.dtype),
        ],
        scratch_shapes=[
            pltpu.VMEM((reqs, depth), jnp.float32),
            pltpu.VMEM(kept.shape, kept.dtype),
            pltpu.SemaphoreType.DMA,
        ],
        compiler_params=pltpu.CompilerParams(vmem_limit_bytes=24 * 1024 * 1024),
        name="output",
    )(source, heads, weight, kept, *pages)


def shards(normed, qkv_weight, out_weight, prefill_pool, page_table, lengths, selected, handoff):
    owners = lax.axis_size("src")
    decoders = lax.axis_size("dst")
    decoder_id = lax.axis_index("dst")
    groups = decoders // KVH
    reqs = normed.shape[0]
    req_group = reqs // groups
    pool = prefill_pool.reshape(prefill_pool.shape[0], *prefill_pool.shape[2:])
    slots, page_len = pool.shape[:2]
    capacity = slots // owners + 1

    packed = pack(handoff, pool, owners, capacity)
    arrived = []
    for k, pages in enumerate(packed):
        arrived.append(lax.ppermute(pages, "src", [(i, i ^ (k + 1)) for i in range(owners)]))

    rows = qkv_weight.shape[0]
    tokens = normed
    if rows % 128:
        row_block = lax.axis_index("src") * decoders + decoder_id
        tokens = lax.dynamic_slice_in_dim(normed, row_block * rows, rows, 1)
    partial = project(tokens, qkv_weight, groups, packed[0])
    live, cosine, sine, source = plan(
        handoff, page_table, lengths, selected, pool.shape[2] // 2, req_group, slots, page_len
    )
    shares = lax.all_to_all(
        partial.reshape((decoders,) + partial.shape[2:]), "dst",
        split_axis=0, concat_axis=0, tiled=True,
    )
    projected = lax.all_gather(jnp.sum(shares, axis=0), "src")
    mine = attend(projected, pool, live, cosine, sine)
    heads = lax.all_gather(mine, "src")
    merged = groups == 1
    if not merged:
        attended = merge(heads).astype(jnp.bfloat16)
        head_dim = attended.shape[1]
        flat = attended.reshape(GRP, req_group, head_dim).transpose(1, 0, 2)
        every = lax.all_gather(flat.reshape(req_group, -1), "dst", axis=0, tiled=True)
        every = every.reshape(groups, KVH, req_group, -1)
        block = lax.dynamic_index_in_dim(every, decoder_id // groups, 1, keepdims=False)
        depth = out_weight.shape[0]
        heads = lax.dynamic_slice_in_dim(
            block.reshape(reqs, -1), (decoder_id % groups) * depth, depth, 1
        )
    outgoing, decode_pool = output(
        source, heads, out_weight, pool, arrived, reqs, decoders, merged
    )
    incoming = lax.all_to_all(outgoing, "dst", split_axis=0, concat_axis=0, tiled=True)
    attn_out = jnp.sum(incoming.astype(jnp.float32), axis=0)
    return attn_out, decode_pool[:, None]


def solution(mesh):
    return jax.shard_map(
        shards,
        mesh=mesh,
        in_specs=(
            P(),
            P(("src", "dst"), None),
            P("dst", "src"),
            P("src", "dst", None, None),
            P(),
            P(),
            P(),
            P(),
        ),
        out_specs=(P(None, "src"), P("src", "dst", None, None)),
        check_vma=False,
    )
```

time: 114 us -> 60.6 us (0.53)
  Pallas kernels: 48.7 us -> 15 us
  local copies, waits for them, and re-layouts: 16.3 us -> 3.28 us
  blocking collectives: 35.7 us -> 28.5 us
  waiting for transfers between devices: 0.01 us -> 2.95 us
  starting transfers between devices: 10.8 us -> 9.13 us
    pallas_call x3 -> x4, Pallas kernels: 48.1 us -> 14.4 us  [the longest x1 4.59 us: output(): pl.pallas_call(functools.partial(output_body, merged), in_specs=[SMEM, VM...]
    unnamed x18 -> x16, local copies, waits for them, and re-layouts: 16.3 us -> 3.28 us
    all_gather x1, blocking collectives: 17 us -> 9.64 us  [shards(): projected = lax.all_gather(jnp.sum(shares, axis=0), 'src')]
    all_to_all x1 -> x0, starting transfers between devices: 3.54 us -> none  [shards(): lax.all_to_all(packed, 'src', split_axis=0, concat_axis=0, tiled=True)]
    all_to_all x1, waiting for transfers between devices: 0.01 us -> 2.94 us  [shards(): lax.all_to_all(partial.reshape((decoders,) + partial.shape[2:]), 'dst', s...]
    ppermute x0 -> x3, starting transfers between devices: none -> 1.85 us  [shards(): lax.ppermute(pages, 'src', [(i, i ^ k + 1) for i in range(owners)])]
  transfers between devices with their start and end apart: 2 -> 4, of which waited for: 0 -> 1; matrix products, arithmetic and copies ran while one was open for 0% -> 0% of each run, Pallas kernels for 30% -> 6%
where the time goes in v2:
time: 60.6 us; the launch traced here: 60.3 us
  blocking collectives  28.5 us (47%)
  Pallas kernels  15 us (25%)
  starting transfers between devices  9.13 us (15%)
  local copies, waits for them, and re-layouts  3.28 us (5%)
  waiting for transfers between devices  2.95 us (5%)
  between operations  0.76 us (1%)
  other arithmetic  0.74 us (1%)
    all_to_all x1, blocking collectives, shards(): lax.all_to_all(outgoing, 'dst', split_axis=0, concat_axis=0, tiled=True)  13.3 us
    all_gather x1, blocking collectives, shards(): projected = lax.all_gather(jnp.sum(shares, axis=0), 'src')  9.64 us
    all_to_all x1, starting transfers between devices, shards(): lax.all_to_all(partial.reshape((decoders,) + partial.shape[2:]), 'dst', s...  7.28 us
    all_gather x1, blocking collectives, shards(): heads = lax.all_gather(mine, 'src')  5.54 us
    pallas_call x1, Pallas kernels, output(): pl.pallas_call(functools.partial(output_body, merged), in_specs=[SMEM, VM...  4.59 us
    pallas_call x1, Pallas kernels, pack(): pl.pallas_call(pack_body, out_shape=[one] * (owners - 1), in_specs=[SMEM,...  3.76 us
    unnamed x16, local copies, waits for them, and re-layouts  3.28 us
    pallas_call x1, Pallas kernels, project(): pl.pallas_call(project_body, in_specs=[VMEM, VMEM, ANY], out_specs=VMEM,...  3.24 us
  transfers between devices with their start and end apart: 4, of which 1 were waited for; matrix products, arithmetic and copies ran while one was open for 0% of the time, Pallas kernels for 6%

profile of v2, /device:TPU:0, one launch (start us, length us, event | category | flops | bytes accessed | tf_op | source)
XLA Modules:
  0.0 60.3 jit_solution(6113097301750913531)
XLA Ops:
  0.6 0.0 slice-start
  0.6 0.0 slice-start.1
  0.7 0.0 slice-start.2
  0.7 0.0 slice-start.3
  0.7 0.0 slice-start.4
  0.7 3.8 %pack.1 = (bf16[9,64,256]{2,1,0:T(8,128)(2,1)}, bf16[9,64,256]{2,1,0:T(8,128)(2,1)}, bf16[9,64,256]{2,1,0:T(8,128)(2,1)}) custom-call(s32[1,128]{1,0:T(1,128)} %handoff.3, bf16[32,64,256]{2,1,0:T(8,128)(2,1)} %bitcast.9), custom_call_target="tpu_custom_call" | custom-call | flops 10000000000 | bytes 33554432 | tf_op jit(solution)/shard_map/pack/pallas_call | solution.py:67
  4.5 0.0 copy-start.1
  4.5 1.5 %slice-done.2 = s8[4194304]{0:T(1024)(128)(4,1)S(1)} async-done(((s8[18874368]{0:T(1024)(128)(4,1)}), s8[4194304]{0:T(1024)(128)(4,1)S(1)}, s32[]{:S(2)}) %slice-start.2) | async-done | bytes 4194328
  6.0 1.2 %slice-done.3 = s8[4194304]{0:T(1024)(128)(4,1)S(1)} async-done(((s8[18874368]{0:T(1024)(128)(4,1)}), s8[4194304]{0:T(1024)(128)(4,1)S(1)}, s32[]{:S(2)}) %slice-start.3) | async-done | bytes 4194328
  7.2 0.6 slice-done.4
  7.8 3.2 %project.1 = f32[1,8,36,128]{3,2,1,0:T(8,128)} custom-call(bf16[2,16384]{1,0:T(2,128)(2,1)S(1)} %copy-done.2, bf16[512,18432]{1,0:T(8,128)(2,1)S(1)} %bitcast.8, bf16[9,64,256]{2,1,0:T(8,128)(2,1)} %get-tuple-element.12._after), custom_call_target="tpu_custom_call" | custom-call | tf_op jit(solution)/shard_map/project/pallas_call | solution.py:106
  11.0 7.3 %all-to-all-start = ((f32[8,36,128]{2,1,0:T(8,128)}), f32[8,36,128]{2,1,0:T(8,128)S(1)}, u32[]{:S(2)}, u32[]{:S(2)}) async-start(f32[8,36,128]{2,1,0:T(8,128)} %bitcast.1), calls=%async_computation | async-start | bytes 327680 | tf_op jit(solution)/shard_map/all_to_all | solution.py:365
  18.3 1.6 %collective-permute-start.1 = (bf16[9,64,256]{2,1,0:T(8,128)(2,1)}, bf16[9,64,256]{2,1,0:T(8,128)(2,1)}, u32[]{:S(2)}, u32[]{:S(2)}) collective-permute-start(bf16[9,64,256]{2,1,0:T(8,128)(2,1)} %get-tuple-element.16), channel_id=1, source_target_pairs={{0,16},{8,24},{16,0},{24,8},{1,17},{9,25},{17,1},{25,9},{2,18},{10... | collective-permute-start | bytes 884744 | tf_op jit(solution)/shard_map/ppermute | solution.py:354
  19.9 0.3 collective-permute-start.2
  20.1 2.8 %plan.1 = (f32[2,2048]{1,0:T(2,128)S(1)}, f32[2,128]{1,0:T(2,128)S(1)}, f32[2,128]{1,0:T(2,128)S(1)}, s32[41]{0:T(128)S(1)}) custom-call(s32[1,128]{1,0:T(1,128)} %handoff.3, s32[2,96]{1,0:T(2,128)} %table.1, s32[2]{0:T(128)} %lengths.1, s32[2,8,32]{2,1,0:T(8,128)} %selected.1, f32[1,128]{1,0:T(1,128)} %constant.6.frequency), custom_call_target="tpu_custom_call" | custom-call | tf_op jit(solution)/shard_map/plan/pallas_call | solution.py:185
  22.9 2.9 %all-to-all-done = f32[8,36,128]{2,1,0:T(8,128)S(1)} async-done(((f32[8,36,128]{2,1,0:T(8,128)}), f32[8,36,128]{2,1,0:T(8,128)S(1)}, u32[]{:S(2)}, u32[]{:S(2)}) %all-to-all-start) | async-done | bytes 147488 | tf_op jit(solution)/shard_map/all_to_all | solution.py:365
  25.9 9.6 %all-gather.2.parts = f32[4,36,128]{2,1,0:T(8,128)S(1)} all-gather(f32[1,36,128]{2,1,0:T(8,128)S(1)} %bitcast.13), channel_id=2, replica_groups=mesh['src'=4,'dst'=8] {'src'}, dimensions={0}, use_global_device_ids=true | all-gather | bytes 92160 | tf_op jit(solution)/shard_map/all_gather | solution.py:369
  35.5 0.6 %attend.1 = f32[32,256]{1,0:T(8,128)S(1)} custom-call(f32[4,36,128]{2,1,0:T(8,128)S(1)} %all-gather.2.parts, bf16[32,64,256]{2,1,0:T(8,128)(2,1)S(1)} %bitcast.10, f32[2,2048]{1,0:T(2,128)S(1)} %get-tuple-element.13.live, f32[2,128]{1,0:T(2,128)S(1)} %get-tuple-element.14.cosine, f32[2,128]{1,0:T(2,128)S(1)} %get-tuple-element.15.sine), custom_call_target="tpu_custom_call" | custom-call | flops 999999995904 | bytes 67108864 | tf_op jit(solution)/shard_map/attend/pallas_call | solution.py:250
  36.1 5.5 %all-gather.1 = f32[128,256]{1,0:T(8,128)S(1)} all-gather(f32[32,256]{1,0:T(8,128)S(1)} %attend.1), channel_id=3, replica_groups=mesh['src'=4,'dst'=8] {'src'}, dimensions={0}, use_global_device_ids=true | all-gather | bytes 163840 | tf_op jit(solution)/shard_map/all_gather | solution.py:371
  41.7 0.0 collective-permute-done.2.rest_2_
  41.7 0.0 collective-permute-done.rest_0_
  41.7 4.6 %output.1 = (bf16[8,2,4096]{2,1,0:T(2,128)(2,1)S(1)}, bf16[32,64,256]{2,1,0:T(8,128)(2,1)}) custom-call(s32[41]{0:T(128)S(1)} %get-tuple-element.11.source, f32[4,32,256]{2,1,0:T(8,128)S(1)} %bitcast.12, bf16[2048,4096]{1,0:T(8,128)(2,1)S(1)} %copy-done, bf16[32,64,256]{2,1,0:T(8,128)(2,1)S(1)} %bitcast.11, ...), custom_call_target="tpu_custom_call" | custom-call | tf_op jit(solution)/shard_map/output/pallas_call | solution.py:322
  46.3 13.3 %all_to_all.10 = bf16[8,2,4096]{2,1,0:T(2,128)(2,1)S(1)} all-to-all(bf16[8,2,4096]{2,1,0:T(2,128)(2,1)S(1)} %get-tuple-element.18), channel_id=1, replica_groups=mesh['src'=4,'dst'=8] {'dst'}, dimensions={0} | all-to-all | bytes 262144 | tf_op jit(solution)/shard_map/all_to_all | solution.py:387
  59.6 0.7 %convert_reduce_fusion = f32[2,4096]{1,0:T(2,128)} fusion(bf16[8,2,4096]{2,1,0:T(2,128)(2,1)S(1)} %all_to_all.10), kind=kLoop, calls=%fused_computation | loop fusion | flops 122880 | bytes 163840 | tf_op jit(solution)/shard_map/reduce_sum | solution.py:388
  (11 shorter events, 0.0 us)
Async XLA Ops:
  0.6 3.8 %slice-start = ((s8[18874368]{0:T(1024)(128)(4,1)}), s8[4194304]{0:T(1024)(128)(4,1)S(1)}, s32[]{:S(2)}) async-start(s8[18874368]{0:T(1024)(128)(4,1)} %bitcast.7), calls=%async_computation.2 | async-start | bytes 8388608
  0.6 3.8 %copy-start.2 = (bf16[2,16384]{1,0:T(2,128)(2,1)S(1)}, bf16[2,16384]{1,0:T(2,128)(2,1)}, u32[]{:S(2)}) copy-start(bf16[2,16384]{1,0:T(2,128)(2,1)} %tokens.1) | copy-start | bytes 196612
  0.6 3.8 %slice-start.1 = ((s8[18874368]{0:T(1024)(128)(4,1)}), s8[4194304]{0:T(1024)(128)(4,1)S(1)}, s32[]{:S(2)}) async-start(s8[18874368]{0:T(1024)(128)(4,1)} %bitcast.7), calls=%async_computation.3 | async-start | bytes 8388608
  0.7 5.3 %slice-start.2 = ((s8[18874368]{0:T(1024)(128)(4,1)}), s8[4194304]{0:T(1024)(128)(4,1)S(1)}, s32[]{:S(2)}) async-start(s8[18874368]{0:T(1024)(128)(4,1)} %bitcast.7), calls=%async_computation.4 | async-start | bytes 8388608
  0.7 6.5 %slice-start.3 = ((s8[18874368]{0:T(1024)(128)(4,1)}), s8[4194304]{0:T(1024)(128)(4,1)S(1)}, s32[]{:S(2)}) async-start(s8[18874368]{0:T(1024)(128)(4,1)} %bitcast.7), calls=%async_computation.5 | async-start | bytes 8388608
  0.7 7.1 %slice-start.4 = ((s8[18874368]{0:T(1024)(128)(4,1)}), s8[2097152]{0:T(1024)(128)(4,1)S(1)}, s32[]{:S(2)}) async-start(s8[18874368]{0:T(1024)(128)(4,1)} %bitcast.7), calls=%async_computation.6 | async-start | bytes 4194304
  4.5 31.0 %copy-start.1 = (bf16[32,1,64,256]{3,2,1,0:T(8,128)(2,1)S(1)}, bf16[32,1,64,256]{3,2,1,0:T(8,128)(2,1)}, u32[]{:S(2)}) copy-start(bf16[32,1,64,256]{3,2,1,0:T(8,128)(2,1)} %param.12) | copy-start | bytes 3145732
  11.0 14.8 %all-to-all-start = ((f32[8,36,128]{2,1,0:T(8,128)}), f32[8,36,128]{2,1,0:T(8,128)S(1)}, u32[]{:S(2)}, u32[]{:S(2)}) async-start(f32[8,36,128]{2,1,0:T(8,128)} %bitcast.1), calls=%async_computation | async-start | bytes 327680 | tf_op jit(solution)/shard_map/all_to_all | solution.py:365
  18.3 23.4 %collective-permute-start = (bf16[9,64,256]{2,1,0:T(8,128)(2,1)}, bf16[9,64,256]{2,1,0:T(8,128)(2,1)}, u32[]{:S(2)}, u32[]{:S(2)}) collective-permute-start(bf16[9,64,256]{2,1,0:T(8,128)(2,1)} %get-tuple-element.12._after), channel_id=1, source_target_pairs={{0,8},{8,0},{16,24},{24,16},{1,9},{9,1},{17,25},{25,17},{2,10},{10... | collective-permute-start | bytes 884744 | tf_op jit(solution)/shard_map/ppermute | solution.py:354
  18.3 23.4 %collective-permute-start.1 = (bf16[9,64,256]{2,1,0:T(8,128)(2,1)}, bf16[9,64,256]{2,1,0:T(8,128)(2,1)}, u32[]{:S(2)}, u32[]{:S(2)}) collective-permute-start(bf16[9,64,256]{2,1,0:T(8,128)(2,1)} %get-tuple-element.16), channel_id=1, source_target_pairs={{0,16},{8,24},{16,0},{24,8},{1,17},{9,25},{17,1},{25,9},{2,18},{10... | collective-permute-start | bytes 884744 | tf_op jit(solution)/shard_map/ppermute | solution.py:354
  19.9 21.8 %collective-permute-start.2 = (bf16[9,64,256]{2,1,0:T(8,128)(2,1)}, bf16[9,64,256]{2,1,0:T(8,128)(2,1)}, u32[]{:S(2)}, u32[]{:S(2)}) collective-permute-start(bf16[9,64,256]{2,1,0:T(8,128)(2,1)} %get-tuple-element.17), channel_id=1, source_target_pairs={{0,24},{8,16},{16,8},{24,0},{1,25},{9,17},{17,9},{25,1},{2,26},{10... | collective-permute-start | bytes 884744 | tf_op jit(solution)/shard_map/ppermute | solution.py:354
  35.5 6.2 %copy-start = (bf16[2048,4096]{1,0:T(8,128)(2,1)S(1)}, bf16[2048,4096]{1,0:T(8,128)(2,1)}, u32[]{:S(2)}) copy-start(bf16[2048,4096]{1,0:T(8,128)(2,1)} %weight.3) | copy-start | bytes 50331652

commit v3 on v2

--- a/solution.py
+++ b/solution.py
@@ -32,14 +32,20 @@
     return np.concatenate([frequency, frequency]).astype(np.float32)
 
 
-def pack_body(handoff, pool, *rest):
-    packed, (count, sem) = rest[:-2], rest[-2:]
+def pack_body(handoff_in, pool_in, *rest):
+    packed, (handoff, count, pool, handoff_sem, pool_sem, page_sem) = rest[:-6], rest[-6:]
     owners = len(packed) + 1
     slots = pool.shape[0]
     group = lax.axis_index("dst") // KVH
     me = lax.axis_index("src")
+    first = pltpu.make_async_copy(handoff_in, handoff, handoff_sem)
+    whole = pltpu.make_async_copy(pool_in, pool, pool_sem)
+    first.start()
+    whole.start()
     for offset in range(owners):
         count[offset] = 0
+    first.wait()
+    whole.wait()
 
     def send(slot, carry):
         offset = handoff[group, me * slots + slot] ^ me
@@ -49,34 +55,42 @@
 
             @pl.when(offset == other)
             def _(other=other):
-                pltpu.make_async_copy(pool.at[slot], packed[other - 1].at[place], sem).start()
+                pltpu.make_async_copy(pool.at[slot], packed[other - 1].at[place], page_sem).start()
 
         return carry
 
     lax.fori_loop(0, slots, send, 0)
 
     def settle(index, carry):
-        pltpu.make_async_copy(pool.at[0], packed[0].at[0], sem).wait()
+        pltpu.make_async_copy(pool.at[0], packed[0].at[0], page_sem).wait()
         return carry
 
     lax.fori_loop(0, slots - count[0], settle, 0)
 
 
-def pack(handoff, pool, owners, capacity):
-    one = pltpu.VMEM((capacity,) + pool.shape[1:], pool.dtype)
+def pack(handoff, pool, owners):
+    slots = pool.shape[0]
+    one = jax.ShapeDtypeStruct((slots // owners + 1,) + pool.shape[1:], pool.dtype)
     return pl.pallas_call(
         pack_body,
         out_shape=[one] * (owners - 1),
-        in_specs=[SMEM, ANY],
-        out_specs=[VMEM] * (owners - 1),
-        scratch_shapes=[pltpu.SMEM((owners,), jnp.int32), pltpu.SemaphoreType.DMA],
+        in_specs=[ANY, ANY],
+        out_specs=[ANY] * (owners - 1),
+        scratch_shapes=[
+            pltpu.SMEM(handoff.shape, jnp.int32),
+            pltpu.SMEM((owners,), jnp.int32),
+            pltpu.VMEM(pool.shape, pool.dtype),
+            pltpu.SemaphoreType.DMA,
+            pltpu.SemaphoreType.DMA,
+            pltpu.SemaphoreType.DMA,
+        ],
         compiler_params=pltpu.CompilerParams(vmem_limit_bytes=4 * 1024 * 1024),
         cost_estimate=pl.CostEstimate(flops=10**10, bytes_accessed=2**25, transcendentals=0),
         name="pack",
     )(near(handoff), near(pool))
 
 
-def project_body(tokens, weight, _after, out):
+def project_body(tokens, weight, _after, out, shares, sem):
     groups, heads, rows, head_dim = out.shape
     parts = GRP + 2
     reqs = rows // parts
@@ -87,28 +101,31 @@
     else:
         values = tokens[...]
     width = parts * head_dim
-    for head in range(heads):
+    for h in range(heads):
         result = jnp.dot(
-            values, weight[:, head * width : (head + 1) * width],
-            preferred_element_type=jnp.float32,
+            values, weight[:, h * width : (h + 1) * width], preferred_element_type=jnp.float32
         )
         for g in range(groups):
             for part in range(parts):
-                out[g, head, part * reqs : (part + 1) * reqs, :] = result[
+                shares[g, h, part * reqs : (part + 1) * reqs, :] = result[
                     g * reqs : (g + 1) * reqs, part * head_dim : (part + 1) * head_dim
                 ]
+            pltpu.make_async_copy(shares.at[g, h], out.at[g, h], sem).start()
+    pltpu.make_async_copy(shares, out, sem).wait()
 
 
 def project(tokens, weight, groups, after):
     reqs = tokens.shape[0] // groups
     parts = GRP + 2
     head_dim = weight.shape[1] // (KVH * parts)
+    share = jax.ShapeDtypeStruct((groups, KVH, parts * reqs, head_dim), jnp.float32)
     return pl.pallas_call(
         project_body,
         in_specs=[VMEM, VMEM, ANY],
-        out_specs=VMEM,
-        out_shape=pltpu.VMEM((groups, KVH, parts * reqs, head_dim), jnp.float32),
-        compiler_params=pltpu.CompilerParams(vmem_limit_bytes=24 * 1024 * 1024),
+        out_specs=ANY,
+        out_shape=share,
+        scratch_shapes=[pltpu.VMEM(share.shape, share.dtype), pltpu.SemaphoreType.DMA],
+        compiler_params=pltpu.CompilerParams(vmem_limit_bytes=8 * 1024 * 1024),
         name="project",
     )(tokens, weight, after)
 
@@ -199,9 +216,7 @@
 
 
 def attend_body(parts, pool, live, cosine, sine, out):
-    total = parts[0]
-    for source in range(1, parts.shape[0]):
-        total = total + parts[source]
+    total = functools.reduce(jnp.add, [parts[i] for i in range(parts.shape[0])])
     head_dim = total.shape[1]
     reqs = live.shape[0]
     rows = GRP * reqs
@@ -271,25 +286,20 @@
     return numerator / denominator
 
 
-def output_body(merged, source, heads, weight, kept, *rest):
-    pages, (out, pool, tokens, stage, sem) = rest[:-5], rest[-5:]
-    copies = out.shape[0]
-    owners = len(pages) + 1
-
-    def keep(index, carry):
-        slot = source[2 * owners + index]
-        pltpu.make_async_copy(kept.at[slot], stage.at[source[owners] + index], sem).start()
-        return carry
-
-    lax.fori_loop(0, source[0], keep, 0)
-    for other in range(1, owners):
-
-        def place(index, carry, other=other):
-            target = stage.at[source[owners + other] + index]
-            pltpu.make_async_copy(pages[other - 1].at[index], target, sem).start()
-            return carry
-
-        lax.fori_loop(0, source[other], place, 0)
+def output_body(merged, source_in, heads, weight, kept_in, *rest):
+    owners = (len(rest) - 4) // 2
+    pages_in, (out, pool, tokens, source, kept), rest = (
+        rest[: owners - 1], rest[owners - 1 : owners + 4], rest[owners + 4 :],
+    )
+    pages, (bulk_sem, page_sem) = rest[: owners - 1], rest[owners - 1 :]
+    bulk = [
+        pltpu.make_async_copy(x, y, bulk_sem.at[i])
+        for i, (x, y) in enumerate(
+            [(source_in, source), (kept_in, kept), *zip(pages_in, pages, strict=True)]
+        )
+    ]
+    for copy in bulk:
+        copy.start()
 
     if merged:
         reqs = tokens.shape[0]
@@ -301,27 +311,47 @@
     else:
         values = heads[...]
 
-    width = weight.shape[1]
-    tile = width // 8 if width % 1024 == 0 else width
-    ordered = pltpu.make_async_copy(stage, pool, sem)
-    for start in range(0, width, tile):
-        if start == width // tile // 2 * tile:
-            pltpu.make_async_copy(kept, stage, sem).wait()
-            ordered.start()
+    def columns(start, tile):
         result = jnp.dot(
             values, weight[:, start : start + tile], preferred_element_type=jnp.float32
         ).astype(out.dtype)
-        for copy in range(copies):
+        for copy in range(out.shape[0]):
             out[copy, :, start : start + tile] = result
 
-    ordered.wait()
+    width = weight.shape[1]
+    tile = width // 8 if width % 1024 == 0 else width
+    starts = range(0, width, tile)
+    for start in starts[: len(starts) // 2]:
+        columns(start, tile)
+
+    for copy in bulk:
+        copy.wait()
+
+    def keep(index, carry):
+        slot = source[2 * owners + index]
+        pltpu.make_async_copy(kept.at[slot], pool.at[source[owners] + index], page_sem).start()
+        return carry
+
+    lax.fori_loop(0, source[0], keep, 0)
+    for other in range(1, owners):
+
+        def place(index, carry, other=other):
+            target = pool.at[source[owners + other] + index]
+            pltpu.make_async_copy(pages[other - 1].at[index], target, page_sem).start()
+            return carry
+
+        lax.fori_loop(0, source[other], place, 0)
+
+    for start in starts[len(starts) // 2 :]:
+        columns(start, tile)
+    pltpu.make_async_copy(kept, pool, page_sem).wait()
 
 
 def output(source, heads, weight, kept, pages, reqs, copies, merged):
     depth, width = weight.shape
     return pl.pallas_call(
         functools.partial(output_body, merged),
-        in_specs=[SMEM, VMEM, VMEM, ANY] + [ANY] * len(pages),
+        in_specs=[ANY, VMEM, VMEM, ANY] + [ANY] * len(pages),
         out_specs=[VMEM, ANY],
         out_shape=[
             jax.ShapeDtypeStruct((copies, reqs, width), jnp.bfloat16),
@@ -329,10 +359,13 @@
         ],
         scratch_shapes=[
             pltpu.VMEM((reqs, depth), jnp.float32),
+            pltpu.SMEM(source.shape, jnp.int32),
             pltpu.VMEM(kept.shape, kept.dtype),
+            *[pltpu.VMEM(page.shape, page.dtype) for page in pages],
+            pltpu.SemaphoreType.DMA((len(pages) + 2,)),
             pltpu.SemaphoreType.DMA,
         ],
-        compiler_params=pltpu.CompilerParams(vmem_limit_bytes=24 * 1024 * 1024),
+        compiler_params=pltpu.CompilerParams(vmem_limit_bytes=12 * 1024 * 1024),
         name="output",
     )(source, heads, weight, kept, *pages)
 
@@ -345,27 +378,22 @@
     reqs = normed.shape[0]
     req_group = reqs // groups
     pool = prefill_pool.reshape(prefill_pool.shape[0], *prefill_pool.shape[2:])
-    slots, page_len = pool.shape[:2]
-    capacity = slots // owners + 1
-
-    packed = pack(handoff, pool, owners, capacity)
-    arrived = []
-    for k, pages in enumerate(packed):
-        arrived.append(lax.ppermute(pages, "src", [(i, i ^ (k + 1)) for i in range(owners)]))
-
     rows = qkv_weight.shape[0]
     tokens = normed
     if rows % 128:
         row_block = lax.axis_index("src") * decoders + decoder_id
         tokens = lax.dynamic_slice_in_dim(normed, row_block * rows, rows, 1)
+    packed = pack(handoff, pool, owners)
+    arrived = []
+    for k, pages in enumerate(packed):
+        arrived.append(lax.ppermute(pages, "src", [(i, i ^ (k + 1)) for i in range(owners)]))
     partial = project(tokens, qkv_weight, groups, packed[0])
     live, cosine, sine, source = plan(
-        handoff, page_table, lengths, selected, pool.shape[2] // 2, req_group, slots, page_len
-    )
-    shares = lax.all_to_all(
-        partial.reshape((decoders,) + partial.shape[2:]), "dst",
-        split_axis=0, concat_axis=0, tiled=True,
-    )
+        handoff, page_table, lengths, selected, pool.shape[2] // 2, req_group, pool.shape[0],
+        pool.shape[1],
+    )
+    partial = partial.reshape((decoders,) + partial.shape[2:])
+    shares = lax.all_to_all(partial, "dst", split_axis=0, concat_axis=0, tiled=True)
     projected = lax.all_gather(jnp.sum(shares, axis=0), "src")
     mine = attend(projected, pool, live, cosine, sine)
     heads = lax.all_gather(mine, "src")

time: 60.6 us -> 58.9 us (0.972)
  Pallas kernels: 15 us -> 11.8 us
  local copies, waits for them, and re-layouts: 3.28 us -> 4.75 us
    pallas_call x3, Pallas kernels: 11.6 us -> 8.47 us  [the longest x1 3.17 us: project(): pl.pallas_call(project_body, in_specs=[VMEM, VMEM, ANY], out_specs=ANY, o...]
    unnamed x16, local copies, waits for them, and re-layouts: 3.28 us -> 4.75 us
where the time goes in v3:
time: 58.9 us; the launch traced here: 58.6 us
  blocking collectives  28.5 us (48%)
  Pallas kernels  11.8 us (20%)
  starting transfers between devices  9.15 us (16%)
  local copies, waits for them, and re-layouts  4.75 us (8%)
  waiting for transfers between devices  2.95 us (5%)
  between operations  0.75 us (1%)
  other arithmetic  0.74 us (1%)
    all_to_all x1, blocking collectives, shards(): lax.all_to_all(outgoing, 'dst', split_axis=0, concat_axis=0, tiled=True)  13.3 us
    all_gather x1, blocking collectives, shards(): projected = lax.all_gather(jnp.sum(shares, axis=0), 'src')  9.64 us
    all_to_all x1, starting transfers between devices, shards(): lax.all_to_all(partial, 'dst', split_axis=0, concat_axis=0, tiled=True)  7.29 us
    all_gather x1, blocking collectives, shards(): heads = lax.all_gather(mine, 'src')  5.54 us
    unnamed x16, local copies, waits for them, and re-layouts  4.75 us
    pallas_call x1, Pallas kernels, project(): pl.pallas_call(project_body, in_specs=[VMEM, VMEM, ANY], out_specs=ANY, o...  3.17 us
    pallas_call x1, Pallas kernels, output(): pl.pallas_call(functools.partial(output_body, merged), in_specs=[ANY, VME...  3.03 us
    all_to_all x1, waiting for transfers between devices, shards(): lax.all_to_all(partial, 'dst', split_axis=0, concat_axis=0, tiled=True)  2.94 us
  transfers between devices with their start and end apart: 4, of which 1 were waited for; matrix products, arithmetic and copies ran while one was open for 0% of the time, Pallas kernels for 6%

profile of v3, /device:TPU:0, one launch (start us, length us, event | category | flops | bytes accessed | tf_op | source)
XLA Modules:
  0.0 58.6 jit_solution(9478861665997233417)
XLA Ops:
  0.7 0.0 slice-start.2
  0.7 0.0 slice-start.3
  0.7 2.3 %pack.1 = (bf16[9,64,256]{2,1,0:T(8,128)(2,1)}, bf16[9,64,256]{2,1,0:T(8,128)(2,1)}, bf16[9,64,256]{2,1,0:T(8,128)(2,1)}) custom-call(s32[1,128]{1,0:T(1,128)} %handoff_in.1, bf16[32,64,256]{2,1,0:T(8,128)(2,1)} %bitcast.9), custom_call_target="tpu_custom_call" | custom-call | flops 10000000000 | bytes 33554432 | tf_op jit(solution)/shard_map/pack/pallas_call | solution.py:74
  3.0 0.0 copy-start.1
  3.0 0.4 slice-done
  3.4 1.3 %slice-done.1 = s8[4194304]{0:T(1024)(128)(4,1)S(1)} async-done(((s8[18874368]{0:T(1024)(128)(4,1)}), s8[4194304]{0:T(1024)(128)(4,1)S(1)}, s32[]{:S(2)}) %slice-start.1) | async-done | bytes 4194328
  4.7 1.2 %slice-done.2 = s8[4194304]{0:T(1024)(128)(4,1)S(1)} async-done(((s8[18874368]{0:T(1024)(128)(4,1)}), s8[4194304]{0:T(1024)(128)(4,1)S(1)}, s32[]{:S(2)}) %slice-start.2) | async-done | bytes 4194328
  5.9 1.2 %slice-done.3 = s8[4194304]{0:T(1024)(128)(4,1)S(1)} async-done(((s8[18874368]{0:T(1024)(128)(4,1)}), s8[4194304]{0:T(1024)(128)(4,1)S(1)}, s32[]{:S(2)}) %slice-start.3) | async-done | bytes 4194328
  7.1 0.6 %slice-done.4 = s8[2097152]{0:T(1024)(128)(4,1)S(1)} async-done(((s8[18874368]{0:T(1024)(128)(4,1)}), s8[2097152]{0:T(1024)(128)(4,1)S(1)}, s32[]{:S(2)}) %slice-start.4) | async-done | bytes 2097176
  7.7 3.2 %project.1 = f32[1,8,36,128]{3,2,1,0:T(8,128)} custom-call(bf16[2,16384]{1,0:T(2,128)(2,1)S(1)} %copy-done.2, bf16[512,18432]{1,0:T(8,128)(2,1)S(1)} %bitcast.8, bf16[9,64,256]{2,1,0:T(8,128)(2,1)} %get-tuple-element.12._after), custom_call_target="tpu_custom_call" | custom-call | tf_op jit(solution)/shard_map/project/pallas_call | solution.py:122
  10.9 7.3 %all-to-all-start = ((f32[8,36,128]{2,1,0:T(8,128)}), f32[8,36,128]{2,1,0:T(8,128)S(1)}, u32[]{:S(2)}, u32[]{:S(2)}) async-start(f32[8,36,128]{2,1,0:T(8,128)} %bitcast.1), calls=%async_computation | async-start | bytes 327680 | tf_op jit(solution)/shard_map/all_to_all | solution.py:396
  18.2 0.0 collective-permute-start
  18.2 1.6 %collective-permute-start.1 = (bf16[9,64,256]{2,1,0:T(8,128)(2,1)}, bf16[9,64,256]{2,1,0:T(8,128)(2,1)}, u32[]{:S(2)}, u32[]{:S(2)}) collective-permute-start(bf16[9,64,256]{2,1,0:T(8,128)(2,1)} %get-tuple-element.16), channel_id=1, source_target_pairs={{0,16},{8,24},{16,0},{24,8},{1,17},{9,25},{17,1},{25,9},{2,18},{10... | collective-permute-start | bytes 884744 | tf_op jit(solution)/shard_map/ppermute | solution.py:389
  19.8 0.3 collective-permute-start.2
  20.0 2.8 %plan.1 = (f32[2,2048]{1,0:T(2,128)S(1)}, f32[2,128]{1,0:T(2,128)S(1)}, f32[2,128]{1,0:T(2,128)S(1)}, s32[41]{0:T(128)S(1)}) custom-call(s32[1,128]{1,0:T(1,128)} %handoff_in.1, s32[2,96]{1,0:T(2,128)} %table.1, s32[2]{0:T(128)} %lengths.1, s32[2,8,32]{2,1,0:T(8,128)} %selected.1, f32[1,128]{1,0:T(1,128)} %constant.6.frequency), custom_call_target="tpu_custom_call" | custom-call | tf_op jit(solution)/shard_map/plan/pallas_call | solution.py:202
  22.8 2.9 %all-to-all-done = f32[8,36,128]{2,1,0:T(8,128)S(1)} async-done(((f32[8,36,128]{2,1,0:T(8,128)}), f32[8,36,128]{2,1,0:T(8,128)S(1)}, u32[]{:S(2)}, u32[]{:S(2)}) %all-to-all-start) | async-done | bytes 147488 | tf_op jit(solution)/shard_map/all_to_all | solution.py:396
  25.8 9.6 %all-gather.2.parts = f32[4,36,128]{2,1,0:T(8,128)S(1)} all-gather(f32[1,36,128]{2,1,0:T(8,128)S(1)} %bitcast.13), channel_id=2, replica_groups=mesh['src'=4,'dst'=8] {'src'}, dimensions={0}, use_global_device_ids=true | all-gather | bytes 92160 | tf_op jit(solution)/shard_map/all_gather | solution.py:397
  35.4 0.6 %attend.1 = f32[32,256]{1,0:T(8,128)S(1)} custom-call(f32[4,36,128]{2,1,0:T(8,128)S(1)} %all-gather.2.parts, bf16[32,64,256]{2,1,0:T(8,128)(2,1)S(1)} %bitcast.10, f32[2,2048]{1,0:T(2,128)S(1)} %get-tuple-element.13.live, f32[2,128]{1,0:T(2,128)S(1)} %get-tuple-element.14.cosine, f32[2,128]{1,0:T(2,128)S(1)} %get-tuple-element.15.sine), custom_call_target="tpu_custom_call" | custom-call | flops 999999995904 | bytes 67108864 | tf_op jit(solution)/shard_map/attend/pallas_call | solution.py:265
  36.0 5.5 %all-gather.1 = f32[128,256]{1,0:T(8,128)S(1)} all-gather(f32[32,256]{1,0:T(8,128)S(1)} %attend.1), channel_id=3, replica_groups=mesh['src'=4,'dst'=8] {'src'}, dimensions={0}, use_global_device_ids=true | all-gather | bytes 163840 | tf_op jit(solution)/shard_map/all_gather | solution.py:399
  41.6 0.0 collective-permute-done.1.rest_1_
  41.6 0.0 collective-permute-done.2.rest_2_
  41.6 3.0 %output.1 = (bf16[8,2,4096]{2,1,0:T(2,128)(2,1)S(1)}, bf16[32,64,256]{2,1,0:T(8,128)(2,1)}) custom-call(s32[41]{0:T(128)S(1)} %get-tuple-element.11.source_in, f32[4,32,256]{2,1,0:T(8,128)S(1)} %bitcast.12, bf16[2048,4096]{1,0:T(8,128)(2,1)S(1)} %copy-done, bf16[32,64,256]{2,1,0:T(8,128)(2,1)S(1)} %bitcast.11, ...), custom_call_target="tpu_custom_call" | custom-call | tf_op jit(solution)/shard_map/output/pallas_call | solution.py:352
  44.6 13.3 %all_to_all.10 = bf16[8,2,4096]{2,1,0:T(2,128)(2,1)S(1)} all-to-all(bf16[8,2,4096]{2,1,0:T(2,128)(2,1)S(1)} %get-tuple-element.18), channel_id=1, replica_groups=mesh['src'=4,'dst'=8] {'dst'}, dimensions={0} | all-to-all | bytes 262144 | tf_op jit(solution)/shard_map/all_to_all | solution.py:415
  57.9 0.7 %convert_reduce_fusion = f32[2,4096]{1,0:T(2,128)} fusion(bf16[8,2,4096]{2,1,0:T(2,128)(2,1)S(1)} %all_to_all.10), kind=kLoop, calls=%fused_computation | loop fusion | flops 122880 | bytes 163840 | tf_op jit(solution)/shard_map/reduce_sum | solution.py:416
  (11 shorter events, 0.0 us)
Async XLA Ops:
  0.6 2.8 %slice-start = ((s8[18874368]{0:T(1024)(128)(4,1)}), s8[4194304]{0:T(1024)(128)(4,1)S(1)}, s32[]{:S(2)}) async-start(s8[18874368]{0:T(1024)(128)(4,1)} %bitcast.7), calls=%async_computation.2 | async-start | bytes 8388608
  0.6 2.8 %copy-start.2 = (bf16[2,16384]{1,0:T(2,128)(2,1)S(1)}, bf16[2,16384]{1,0:T(2,128)(2,1)}, u32[]{:S(2)}) copy-start(bf16[2,16384]{1,0:T(2,128)(2,1)} %tokens.1) | copy-start | bytes 196612
  0.6 4.1 %slice-start.1 = ((s8[18874368]{0:T(1024)(128)(4,1)}), s8[4194304]{0:T(1024)(128)(4,1)S(1)}, s32[]{:S(2)}) async-start(s8[18874368]{0:T(1024)(128)(4,1)} %bitcast.7), calls=%async_computation.3 | async-start | bytes 8388608
  0.7 5.2 %slice-start.2 = ((s8[18874368]{0:T(1024)(128)(4,1)}), s8[4194304]{0:T(1024)(128)(4,1)S(1)}, s32[]{:S(2)}) async-start(s8[18874368]{0:T(1024)(128)(4,1)} %bitcast.7), calls=%async_computation.4 | async-start | bytes 8388608
  0.7 6.4 %slice-start.3 = ((s8[18874368]{0:T(1024)(128)(4,1)}), s8[4194304]{0:T(1024)(128)(4,1)S(1)}, s32[]{:S(2)}) async-start(s8[18874368]{0:T(1024)(128)(4,1)} %bitcast.7), calls=%async_computation.5 | async-start | bytes 8388608
  0.7 7.0 %slice-start.4 = ((s8[18874368]{0:T(1024)(128)(4,1)}), s8[2097152]{0:T(1024)(128)(4,1)S(1)}, s32[]{:S(2)}) async-start(s8[18874368]{0:T(1024)(128)(4,1)} %bitcast.7), calls=%async_computation.6 | async-start | bytes 4194304
  3.0 32.4 %copy-start.1 = (bf16[32,1,64,256]{3,2,1,0:T(8,128)(2,1)S(1)}, bf16[32,1,64,256]{3,2,1,0:T(8,128)(2,1)}, u32[]{:S(2)}) copy-start(bf16[32,1,64,256]{3,2,1,0:T(8,128)(2,1)} %param.12) | copy-start | bytes 3145732
  10.9 14.9 %all-to-all-start = ((f32[8,36,128]{2,1,0:T(8,128)}), f32[8,36,128]{2,1,0:T(8,128)S(1)}, u32[]{:S(2)}, u32[]{:S(2)}) async-start(f32[8,36,128]{2,1,0:T(8,128)} %bitcast.1), calls=%async_computation | async-start | bytes 327680 | tf_op jit(solution)/shard_map/all_to_all | solution.py:396
  18.2 23.4 %collective-permute-start = (bf16[9,64,256]{2,1,0:T(8,128)(2,1)}, bf16[9,64,256]{2,1,0:T(8,128)(2,1)}, u32[]{:S(2)}, u32[]{:S(2)}) collective-permute-start(bf16[9,64,256]{2,1,0:T(8,128)(2,1)} %get-tuple-element.12._after), channel_id=1, source_target_pairs={{0,8},{8,0},{16,24},{24,16},{1,9},{9,1},{17,25},{25,17},{2,10},{10... | collective-permute-start | bytes 884744 | tf_op jit(solution)/shard_map/ppermute | solution.py:389
  18.2 23.4 %collective-permute-start.1 = (bf16[9,64,256]{2,1,0:T(8,128)(2,1)}, bf16[9,64,256]{2,1,0:T(8,128)(2,1)}, u32[]{:S(2)}, u32[]{:S(2)}) collective-permute-start(bf16[9,64,256]{2,1,0:T(8,128)(2,1)} %get-tuple-element.16), channel_id=1, source_target_pairs={{0,16},{8,24},{16,0},{24,8},{1,17},{9,25},{17,1},{25,9},{2,18},{10... | collective-permute-start | bytes 884744 | tf_op jit(solution)/shard_map/ppermute | solution.py:389
  19.8 21.8 %collective-permute-start.2 = (bf16[9,64,256]{2,1,0:T(8,128)(2,1)}, bf16[9,64,256]{2,1,0:T(8,128)(2,1)}, u32[]{:S(2)}, u32[]{:S(2)}) collective-permute-start(bf16[9,64,256]{2,1,0:T(8,128)(2,1)} %get-tuple-element.17), channel_id=1, source_target_pairs={{0,24},{8,16},{16,8},{24,0},{1,25},{9,17},{17,9},{25,1},{2,26},{10... | collective-permute-start | bytes 884744 | tf_op jit(solution)/shard_map/ppermute | solution.py:389
  35.4 6.2 %copy-start = (bf16[2048,4096]{1,0:T(8,128)(2,1)S(1)}, bf16[2048,4096]{1,0:T(8,128)(2,1)}, u32[]{:S(2)}) copy-start(bf16[2048,4096]{1,0:T(8,128)(2,1)} %weight.3) | copy-start | bytes 50331652

commit v4 on v3

--- a/solution.py
+++ b/solution.py
@@ -32,20 +32,33 @@
     return np.concatenate([frequency, frequency]).astype(np.float32)
 
 
-def pack_body(handoff_in, pool_in, *rest):
-    packed, (handoff, count, pool, handoff_sem, pool_sem, page_sem) = rest[:-6], rest[-6:]
-    owners = len(packed) + 1
-    slots = pool.shape[0]
+def prepare_body(
+    reqs, handoff_in, table_in, lengths_in, selected_in, frequency_in, pool_in, *rest
+):
+    slots, page_len, width = pool_in.shape
+    head_dim = width // 2
+    owners = handoff_in.shape[1] // slots
+    packed, rest = rest[: owners - 1], rest[owners - 1 :]
+    live_out, turn_out, source_out, *rest = rest
+    handoff, table, lengths, selected, limit, count, source, *rest = rest
+    frequency, pool, live, turns, small_sem, pool_sem, page_sem, fact_sem = rest
+    me = lax.axis_index("src")
     group = lax.axis_index("dst") // KVH
-    me = lax.axis_index("src")
-    first = pltpu.make_async_copy(handoff_in, handoff, handoff_sem)
-    whole = pltpu.make_async_copy(pool_in, pool, pool_sem)
-    first.start()
-    whole.start()
+    head = lax.axis_index("dst") % KVH
+
+    moves = [
+        (handoff_in, handoff), (table_in, table), (lengths_in, lengths), (selected_in, selected),
+        (frequency_in, frequency),
+    ]
+    small = [pltpu.make_async_copy(x, y, small_sem.at[i]) for i, (x, y) in enumerate(moves)]
+    pool_copy = pltpu.make_async_copy(pool_in, pool, pool_sem)
+    for copy in (*small, pool_copy):
+        copy.start()
+
     for offset in range(owners):
         count[offset] = 0
-    first.wait()
-    whole.wait()
+    small[0].wait()
+    pool_copy.wait()
 
     def send(slot, carry):
         offset = handoff[group, me * slots + slot] ^ me
@@ -60,6 +73,70 @@
         return carry
 
     lax.fori_loop(0, slots, send, 0)
+    for copy in small[1:]:
+        copy.wait()
+
+    def clear(index, carry):
+        limit[index] = 0
+        return carry
+
+    lax.fori_loop(0, reqs * slots, clear, 0, unroll=16)
+    for r in range(reqs):
+        length = lengths[group * reqs + r]
+
+        def mark(entry, carry, r=r, length=length):
+            page = selected[group * reqs + r, head, entry]
+            local = table[group * reqs + r, page] - me * slots
+            mine = (local >= 0) & (local < slots)
+            limit[jnp.where(mine, r * slots + local, reqs * slots)] = length - page * page_len
+            return carry
+
+        lax.fori_loop(0, selected.shape[2], mark, 0, unroll=8)
+
+    lane = lax.broadcasted_iota(jnp.int32, (1, 128), 1)
+    per = 128 // page_len
+    for r in range(reqs):
+        for chunk in range(slots // per):
+            bound = jnp.full((1, 128), limit[r * slots + chunk * per], jnp.int32)
+            for k in range(1, per):
+                bound = jnp.where(lane >= k * page_len, limit[r * slots + chunk * per + k], bound)
+            live[r : r + 1, chunk * 128 : (chunk + 1) * 128] = jnp.where(
+                lane % page_len < bound, 1.0, 0.0
+            )
+
+    row = lax.broadcasted_iota(jnp.int32, (reqs, head_dim), 0)
+    place = lax.broadcasted_iota(jnp.int32, (reqs, head_dim), 1)
+    position = jnp.zeros((reqs, head_dim), jnp.float32)
+    for r in range(reqs):
+        position = jnp.where(row == r, lengths[group * reqs + r].astype(jnp.float32), position)
+    angle = frequency[...] * position
+    turns[0] = jnp.cos(angle)
+    sine = jnp.sin(angle)
+    turns[1] = jnp.where(place < head_dim // 2, -sine, sine)
+
+    def owner_pages(owner, filled):
+        own = owner == me
+        source[owners + (owner ^ me)] = filled
+
+        def look(slot, taken):
+            hit = handoff[group, owner * slots + slot] == me
+            source[2 * owners + jnp.where(hit & own, taken, slots)] = slot
+            return taken + hit.astype(jnp.int32)
+
+        taken = lax.fori_loop(0, slots, look, 0, unroll=8)
+        source[owner ^ me] = taken
+        return filled + taken
+
+    lax.fori_loop(0, owners, owner_pages, 0)
+    facts = [
+        pltpu.make_async_copy(x, y, fact_sem.at[i])
+        for i, (x, y) in enumerate([(live, live_out), (turns, turn_out), (source, source_out)])
+    ]
+    for copy in facts:
+        copy.start()
+
+    for copy in facts:
+        copy.wait()
 
     def settle(index, carry):
         pltpu.make_async_copy(pool.at[0], packed[0].at[0], page_sem).wait()
@@ -68,29 +145,42 @@
     lax.fori_loop(0, slots - count[0], settle, 0)
 
 
-def pack(handoff, pool, owners):
-    slots = pool.shape[0]
-    one = jax.ShapeDtypeStruct((slots // owners + 1,) + pool.shape[1:], pool.dtype)
-    return pl.pallas_call(
-        pack_body,
-        out_shape=[one] * (owners - 1),
-        in_specs=[ANY, ANY],
-        out_specs=[ANY] * (owners - 1),
-        scratch_shapes=[
-            pltpu.SMEM(handoff.shape, jnp.int32),
+def prepare(handoff, table, lengths, selected, pool, reqs, owners):
+    slots, page_len, width = pool.shape
+    head_dim = width // 2
+    frequency = jnp.asarray(frequencies(head_dim))[None]
+    page = jax.ShapeDtypeStruct((slots // owners + 1, page_len, width), pool.dtype)
+    live = jax.ShapeDtypeStruct((reqs, slots * page_len), jnp.float32)
+    turns = jax.ShapeDtypeStruct((2, reqs, head_dim), jnp.float32)
+    source = jax.ShapeDtypeStruct((2 * owners + slots + 1,), jnp.int32)
+    integers = [handoff, table, lengths, selected]
+    *packed, live, turns, source = pl.pallas_call(
+        functools.partial(prepare_body, reqs),
+        in_specs=[ANY] * 6,
+        out_specs=[ANY] * (owners + 2),
+        out_shape=[page] * (owners - 1) + [live, turns, source],
+        scratch_shapes=[pltpu.SMEM(a.shape, jnp.int32) for a in integers]
+        + [
+            pltpu.SMEM((reqs * slots + 1,), jnp.int32),
             pltpu.SMEM((owners,), jnp.int32),
+            pltpu.SMEM(source.shape, jnp.int32),
+            pltpu.VMEM(frequency.shape, jnp.float32),
             pltpu.VMEM(pool.shape, pool.dtype),
+            pltpu.VMEM(live.shape, live.dtype),
+            pltpu.VMEM(turns.shape, turns.dtype),
+            pltpu.SemaphoreType.DMA((5,)),
             pltpu.SemaphoreType.DMA,
             pltpu.SemaphoreType.DMA,
-            pltpu.SemaphoreType.DMA,
+            pltpu.SemaphoreType.DMA((3,)),
         ],
         compiler_params=pltpu.CompilerParams(vmem_limit_bytes=4 * 1024 * 1024),
         cost_estimate=pl.CostEstimate(flops=10**10, bytes_accessed=2**25, transcendentals=0),
-        name="pack",
-    )(near(handoff), near(pool))
-
-
-def project_body(tokens, weight, _after, out, shares, sem):
+        name="prepare",
+    )(*map(near, integers), near(frequency), near(pool))
+    return packed, live, turns, source
+
+
+def project_body(tokens, weight, _after, out):
     groups, heads, rows, head_dim = out.shape
     parts = GRP + 2
     reqs = rows // parts
@@ -107,115 +197,26 @@
         )
         for g in range(groups):
             for part in range(parts):
-                shares[g, h, part * reqs : (part + 1) * reqs, :] = result[
+                out[g, h, part * reqs : (part + 1) * reqs, :] = result[
                     g * reqs : (g + 1) * reqs, part * head_dim : (part + 1) * head_dim
                 ]
-            pltpu.make_async_copy(shares.at[g, h], out.at[g, h], sem).start()
-    pltpu.make_async_copy(shares, out, sem).wait()
 
 
 def project(tokens, weight, groups, after):
     reqs = tokens.shape[0] // groups
     parts = GRP + 2
     head_dim = weight.shape[1] // (KVH * parts)
-    share = jax.ShapeDtypeStruct((groups, KVH, parts * reqs, head_dim), jnp.float32)
     return pl.pallas_call(
         project_body,
         in_specs=[VMEM, VMEM, ANY],
-        out_specs=ANY,
-        out_shape=share,
-        scratch_shapes=[pltpu.VMEM(share.shape, share.dtype), pltpu.SemaphoreType.DMA],
+        out_specs=VMEM,
+        out_shape=jax.ShapeDtypeStruct((groups, KVH, parts * reqs, head_dim), jnp.float32),
         compiler_params=pltpu.CompilerParams(vmem_limit_bytes=8 * 1024 * 1024),
         name="project",
     )(tokens, weight, after)
 
 
-def plan_body(
-    page_len, slots, handoff, table, lengths, selected, frequency, live, cosine, sine, source, limit
-):
-    reqs, head_dim = cosine.shape
-    me = lax.axis_index("src")
-    group = lax.axis_index("dst") // KVH
-    head = lax.axis_index("dst") % KVH
-
-    def clear(index, carry):
-        limit[index] = 0
-        return carry
-
-    lax.fori_loop(0, reqs * slots, clear, 0, unroll=16)
-    for r in range(reqs):
-        length = lengths[group * reqs + r]
-
-        def mark(entry, carry, r=r, length=length):
-            page = selected[group * reqs + r, head, entry]
-            slot = table[group * reqs + r, page]
-            local = slot - me * slots
-            mine = (local >= 0) & (local < slots)
-            place = jnp.where(mine, r * slots + local, reqs * slots)
-            limit[place] = length - page * page_len
-            return carry
-
-        lax.fori_loop(0, selected.shape[2], mark, 0, unroll=8)
-
-    lane = lax.broadcasted_iota(jnp.int32, (1, 128), 1)
-    per = 128 // page_len
-    for r in range(reqs):
-        for chunk in range(slots // per):
-            bound = jnp.full((1, 128), limit[r * slots + chunk * per], jnp.int32)
-            for k in range(1, per):
-                bound = jnp.where(lane >= k * page_len, limit[r * slots + chunk * per + k], bound)
-            live[r : r + 1, chunk * 128 : (chunk + 1) * 128] = jnp.where(
-                lane % page_len < bound, 1.0, 0.0
-            )
-
-    row = lax.broadcasted_iota(jnp.int32, (reqs, head_dim), 0)
-    place = lax.broadcasted_iota(jnp.int32, (reqs, head_dim), 1)
-    position = jnp.zeros((reqs, head_dim), jnp.float32)
-    for r in range(reqs):
-        position = jnp.where(row == r, lengths[group * reqs + r].astype(jnp.float32), position)
-    angle = frequency[...] * position
-    cosine[...] = jnp.cos(angle)
-    turn = jnp.sin(angle)
-    sine[...] = jnp.where(place < head_dim // 2, -turn, turn)
-
-    owners = handoff.shape[1] // slots
-
-    def owner_pages(owner, filled):
-        own = owner == me
-        source[owners + (owner ^ me)] = filled
-
-        def look(slot, taken):
-            hit = handoff[group, owner * slots + slot] == me
-            source[2 * owners + jnp.where(hit & own, taken, slots)] = slot
-            return taken + hit.astype(jnp.int32)
-
-        taken = lax.fori_loop(0, slots, look, 0, unroll=8)
-        source[owner ^ me] = taken
-        return filled + taken
-
-    lax.fori_loop(0, owners, owner_pages, 0)
-
-
-def plan(handoff, table, lengths, selected, head_dim, reqs, slots, page_len):
-    owners = handoff.shape[1] // slots
-    frequency = jnp.asarray(frequencies(head_dim))[None]
-    return pl.pallas_call(
-        functools.partial(plan_body, page_len, slots),
-        in_specs=[SMEM] * 4 + [VMEM],
-        out_specs=[VMEM] * 3 + [SMEM],
-        out_shape=[
-            jax.ShapeDtypeStruct((reqs, slots * page_len), jnp.float32),
-            jax.ShapeDtypeStruct((reqs, head_dim), jnp.float32),
-            jax.ShapeDtypeStruct((reqs, head_dim), jnp.float32),
-            jax.ShapeDtypeStruct((2 * owners + slots + 1,), jnp.int32),
-        ],
-        scratch_shapes=[pltpu.SMEM((reqs * slots + 1,), jnp.int32)],
-        compiler_params=pltpu.CompilerParams(vmem_limit_bytes=2 * 1024 * 1024),
-        name="plan",
-    )(near(handoff), near(table), near(lengths), near(selected), near(frequency))
-
-
-def attend_body(parts, pool, live, cosine, sine, out):
+def attend_body(parts, pool, live, turns, out):
     total = functools.reduce(jnp.add, [parts[i] for i in range(parts.shape[0])])
     head_dim = total.shape[1]
     reqs = live.shape[0]
@@ -229,9 +230,9 @@
         return wide
 
     turned = total[: rows + reqs]
-    turned = turned * per_row(cosine[...], rows + reqs) + pltpu.roll(
+    turned = turned * per_row(turns[0], rows + reqs) + pltpu.roll(
         turned, head_dim // 2, 1
-    ) * per_row(sine[...], rows + reqs)
+    ) * per_row(turns[1], rows + reqs)
     queries = (turned[:rows] * head_dim ** (-0.5)).astype(jnp.bfloat16)
     key_new = per_row(turned[rows:], rows)
     value_new = per_row(total[rows + reqs :], rows)
@@ -260,17 +261,17 @@
     out[:, head_dim:] = jnp.where(lane < head_dim // 2, top, total_weight)
 
 
-def attend(parts, pool, live, cosine, sine):
+def attend(parts, pool, live, turns):
     reqs = live.shape[0]
     return pl.pallas_call(
         attend_body,
         out_shape=jax.ShapeDtypeStruct((GRP * reqs, pool.shape[2]), jnp.float32),
-        in_specs=[VMEM] * 5,
+        in_specs=[VMEM] * 4,
         out_specs=VMEM,
         compiler_params=pltpu.CompilerParams(vmem_limit_bytes=16 * 1024 * 1024),
         cost_estimate=pl.CostEstimate(flops=10**12, bytes_accessed=2**26, transcendentals=0),
         name="attend",
-    )(parts, pool, live, cosine, sine)
+    )(parts, pool, live, turns)
 
 
 def merge(parts):
@@ -383,19 +384,17 @@
     if rows % 128:
         row_block = lax.axis_index("src") * decoders + decoder_id
         tokens = lax.dynamic_slice_in_dim(normed, row_block * rows, rows, 1)
-    packed = pack(handoff, pool, owners)
+    packed, live, turns, source = prepare(
+        handoff, page_table, lengths, selected, pool, req_group, owners
+    )
     arrived = []
     for k, pages in enumerate(packed):
         arrived.append(lax.ppermute(pages, "src", [(i, i ^ (k + 1)) for i in range(owners)]))
     partial = project(tokens, qkv_weight, groups, packed[0])
-    live, cosine, sine, source = plan(
-        handoff, page_table, lengths, selected, pool.shape[2] // 2, req_group, pool.shape[0],
-        pool.shape[1],
-    )
     partial = partial.reshape((decoders,) + partial.shape[2:])
     shares = lax.all_to_all(partial, "dst", split_axis=0, concat_axis=0, tiled=True)
     projected = lax.all_gather(jnp.sum(shares, axis=0), "src")
-    mine = attend(projected, pool, live, cosine, sine)
+    mine = attend(projected, pool, live, turns)
     heads = lax.all_gather(mine, "src")
     merged = groups == 1
     if not merged:

time: 58.9 us -> 59 us (level)
  waiting for transfers between devices: 2.95 us -> 5.71 us
  local copies, waits for them, and re-layouts: 4.75 us -> 3.31 us
  Pallas kernels: 11.8 us -> 10.6 us
    all_to_all x1, waiting for transfers between devices: 2.94 us -> 5.7 us  [shards(): lax.all_to_all(partial, 'dst', split_axis=0, concat_axis=0, tiled=True)]
    unnamed x16, local copies, waits for them, and re-layouts: 4.75 us -> 3.31 us
    pallas_call x3 -> x2, Pallas kernels: 8.19 us -> 6.94 us  [the longest x1 3.71 us: prepare(): pl.pallas_call(functools.partial(prepare_body, reqs), in_specs=[ANY] * 6,...]
  transfers between devices with their start and end apart: 4 -> 4, of which waited for: 1 -> 1; matrix products, arithmetic and copies ran while one was open for 0% -> 0% of each run, Pallas kernels for 6% -> 1%
where the time goes in v4:
time: 59 us; the launch traced here: 58.7 us
  blocking collectives  28.5 us (48%)
  Pallas kernels  10.6 us (18%)
  starting transfers between devices  9.13 us (15%)
  waiting for transfers between devices  5.71 us (10%)
  local copies, waits for them, and re-layouts  3.31 us (6%)
  between operations  0.75 us (1%)
  other arithmetic  0.74 us (1%)
    all_to_all x1, blocking collectives, shards(): lax.all_to_all(outgoing, 'dst', split_axis=0, concat_axis=0, tiled=True)  13.3 us
    all_gather x1, blocking collectives, shards(): projected = lax.all_gather(jnp.sum(shares, axis=0), 'src')  9.64 us
    all_to_all x1, starting transfers between devices, shards(): lax.all_to_all(partial, 'dst', split_axis=0, concat_axis=0, tiled=True)  7.28 us
    all_to_all x1, waiting for transfers between devices, shards(): lax.all_to_all(partial, 'dst', split_axis=0, concat_axis=0, tiled=True)  5.7 us
    all_gather x1, blocking collectives, shards(): heads = lax.all_gather(mine, 'src')  5.54 us
    pallas_call x1, Pallas kernels, prepare(): pl.pallas_call(functools.partial(prepare_body, reqs), in_specs=[ANY] * 6,...  3.71 us
    unnamed x16, local copies, waits for them, and re-layouts  3.31 us
    pallas_call x1, Pallas kernels, project(): pl.pallas_call(project_body, in_specs=[VMEM, VMEM, ANY], out_specs=VMEM,...  3.24 us
  transfers between devices with their start and end apart: 4, of which 1 were waited for; matrix products, arithmetic and copies ran while one was open for 0% of the time, Pallas kernels for 1%

profile of v4, /device:TPU:0, one launch (start us, length us, event | category | flops | bytes accessed | tf_op | source)
XLA Modules:
  0.0 58.7 jit_solution(1611528316083620625)
XLA Ops:
  0.6 0.0 slice-start
  0.7 0.0 slice-start.1
  0.7 0.0 slice-start.2
  0.7 0.0 slice-start.4
  0.7 3.7 %prepare.1 = (bf16[9,64,256]{2,1,0:T(8,128)(2,1)}, bf16[9,64,256]{2,1,0:T(8,128)(2,1)}, bf16[9,64,256]{2,1,0:T(8,128)(2,1)}, f32[2,2048]{1,0:T(2,128)S(1)}, f32[2,2,128]{2,1,0:T(2,128)S(1)}, /*index=5*/s32[41]{0:T(128)S(1)}) custom-call(s32[1,128]{1,0:T(1,128)} %handoff_in.1, s32[2,96]{1,0:T(2,128)} %table_in.1, s32[2]{0:T(128)} %lengths_in.1, ...), custom_call_target="tpu_custom_call" | custom-call | flops 10000000000 | bytes 33554432 | tf_op jit(solution)/shard_map/prepare/pallas_call | solution.py:157
  4.4 0.0 copy-start.1
  4.4 0.3 slice-done.1
  4.7 1.2 %slice-done.2 = s8[4194304]{0:T(1024)(128)(4,1)S(1)} async-done(((s8[18874368]{0:T(1024)(128)(4,1)}), s8[4194304]{0:T(1024)(128)(4,1)S(1)}, s32[]{:S(2)}) %slice-start.2) | async-done | bytes 4194328
  5.9 1.2 %slice-done.3 = s8[4194304]{0:T(1024)(128)(4,1)S(1)} async-done(((s8[18874368]{0:T(1024)(128)(4,1)}), s8[4194304]{0:T(1024)(128)(4,1)S(1)}, s32[]{:S(2)}) %slice-start.3) | async-done | bytes 4194328
  7.1 0.6 %slice-done.4 = s8[2097152]{0:T(1024)(128)(4,1)S(1)} async-done(((s8[18874368]{0:T(1024)(128)(4,1)}), s8[2097152]{0:T(1024)(128)(4,1)S(1)}, s32[]{:S(2)}) %slice-start.4) | async-done | bytes 2097176
  7.7 3.2 %project.1 = f32[1,8,36,128]{3,2,1,0:T(8,128)} custom-call(bf16[2,16384]{1,0:T(2,128)(2,1)S(1)} %copy-done.2, bf16[512,18432]{1,0:T(8,128)(2,1)S(1)} %bitcast.8, bf16[9,64,256]{2,1,0:T(8,128)(2,1)} %get-tuple-element.11._after), custom_call_target="tpu_custom_call" | custom-call | tf_op jit(solution)/shard_map/project/pallas_call | solution.py:209
  11.0 7.3 %all-to-all-start = ((f32[8,36,128]{2,1,0:T(8,128)}), f32[8,36,128]{2,1,0:T(8,128)S(1)}, u32[]{:S(2)}, u32[]{:S(2)}) async-start(f32[8,36,128]{2,1,0:T(8,128)} %bitcast.1), calls=%async_computation | async-start | bytes 327680 | tf_op jit(solution)/shard_map/all_to_all | solution.py:395
  18.2 0.0 collective-permute-start
  18.3 1.6 %collective-permute-start.1 = (bf16[9,64,256]{2,1,0:T(8,128)(2,1)}, bf16[9,64,256]{2,1,0:T(8,128)(2,1)}, u32[]{:S(2)}, u32[]{:S(2)}) collective-permute-start(bf16[9,64,256]{2,1,0:T(8,128)(2,1)} %get-tuple-element.14), channel_id=1, source_target_pairs={{0,16},{8,24},{16,0},{24,8},{1,17},{9,25},{17,1},{25,9},{2,18},{10... | collective-permute-start | bytes 884744 | tf_op jit(solution)/shard_map/ppermute | solution.py:392
  19.8 0.3 collective-permute-start.2
  20.1 5.7 %all-to-all-done = f32[8,36,128]{2,1,0:T(8,128)S(1)} async-done(((f32[8,36,128]{2,1,0:T(8,128)}), f32[8,36,128]{2,1,0:T(8,128)S(1)}, u32[]{:S(2)}, u32[]{:S(2)}) %all-to-all-start) | async-done | bytes 147488 | tf_op jit(solution)/shard_map/all_to_all | solution.py:395
  25.8 9.6 %all-gather.2.parts = f32[4,36,128]{2,1,0:T(8,128)S(1)} all-gather(f32[1,36,128]{2,1,0:T(8,128)S(1)} %bitcast.13), channel_id=2, replica_groups=mesh['src'=4,'dst'=8] {'src'}, dimensions={0}, use_global_device_ids=true | all-gather | bytes 92160 | tf_op jit(solution)/shard_map/all_gather | solution.py:396
  35.5 0.6 %attend.1 = f32[32,256]{1,0:T(8,128)S(1)} custom-call(f32[4,36,128]{2,1,0:T(8,128)S(1)} %all-gather.2.parts, bf16[32,64,256]{2,1,0:T(8,128)(2,1)S(1)} %bitcast.10, f32[2,2048]{1,0:T(2,128)S(1)} %get-tuple-element.12.live, f32[2,2,128]{2,1,0:T(2,128)S(1)} %get-tuple-element.13.turns), custom_call_target="tpu_custom_call" | custom-call | flops 999999995904 | bytes 67108864 | tf_op jit(solution)/shard_map/attend/pallas_call | solution.py:266
  36.1 5.5 %all-gather.1 = f32[128,256]{1,0:T(8,128)S(1)} all-gather(f32[32,256]{1,0:T(8,128)S(1)} %attend.1), channel_id=3, replica_groups=mesh['src'=4,'dst'=8] {'src'}, dimensions={0}, use_global_device_ids=true | all-gather | bytes 163840 | tf_op jit(solution)/shard_map/all_gather | solution.py:398
  41.6 0.0 collective-permute-done.2.rest_2_
  41.6 0.0 collective-permute-done.rest_0_
  41.6 3.0 %output.1 = (bf16[8,2,4096]{2,1,0:T(2,128)(2,1)S(1)}, bf16[32,64,256]{2,1,0:T(8,128)(2,1)}) custom-call(s32[41]{0:T(128)S(1)} %get-tuple-element.10.source_in, f32[4,32,256]{2,1,0:T(8,128)S(1)} %bitcast.12, bf16[2048,4096]{1,0:T(8,128)(2,1)S(1)} %copy-done, bf16[32,64,256]{2,1,0:T(8,128)(2,1)S(1)} %bitcast.11, ...), custom_call_target="tpu_custom_call" | custom-call | tf_op jit(solution)/shard_map/output/pallas_call | solution.py:353
  44.7 13.3 %all_to_all.10 = bf16[8,2,4096]{2,1,0:T(2,128)(2,1)S(1)} all-to-all(bf16[8,2,4096]{2,1,0:T(2,128)(2,1)S(1)} %get-tuple-element.16), channel_id=1, replica_groups=mesh['src'=4,'dst'=8] {'dst'}, dimensions={0} | all-to-all | bytes 262144 | tf_op jit(solution)/shard_map/all_to_all | solution.py:414
  58.0 0.7 %convert_reduce_fusion = f32[2,4096]{1,0:T(2,128)} fusion(bf16[8,2,4096]{2,1,0:T(2,128)(2,1)S(1)} %all_to_all.10), kind=kLoop, calls=%fused_computation | loop fusion | flops 122880 | bytes 163840 | tf_op jit(solution)/shard_map/reduce_sum | solution.py:415
  (10 shorter events, 0.0 us)
Async XLA Ops:
  0.6 3.8 %slice-start = ((s8[18874368]{0:T(1024)(128)(4,1)}), s8[4194304]{0:T(1024)(128)(4,1)S(1)}, s32[]{:S(2)}) async-start(s8[18874368]{0:T(1024)(128)(4,1)} %bitcast.7), calls=%async_computation.2 | async-start | bytes 8388608
  0.6 3.8 %copy-start.2 = (bf16[2,16384]{1,0:T(2,128)(2,1)S(1)}, bf16[2,16384]{1,0:T(2,128)(2,1)}, u32[]{:S(2)}) copy-start(bf16[2,16384]{1,0:T(2,128)(2,1)} %tokens.1) | copy-start | bytes 196612
  0.7 4.1 %slice-start.1 = ((s8[18874368]{0:T(1024)(128)(4,1)}), s8[4194304]{0:T(1024)(128)(4,1)S(1)}, s32[]{:S(2)}) async-start(s8[18874368]{0:T(1024)(128)(4,1)} %bitcast.7), calls=%async_computation.3 | async-start | bytes 8388608
  0.7 5.3 %slice-start.2 = ((s8[18874368]{0:T(1024)(128)(4,1)}), s8[4194304]{0:T(1024)(128)(4,1)S(1)}, s32[]{:S(2)}) async-start(s8[18874368]{0:T(1024)(128)(4,1)} %bitcast.7), calls=%async_computation.4 | async-start | bytes 8388608
  0.7 6.5 %slice-start.3 = ((s8[18874368]{0:T(1024)(128)(4,1)}), s8[4194304]{0:T(1024)(128)(4,1)S(1)}, s32[]{:S(2)}) async-start(s8[18874368]{0:T(1024)(128)(4,1)} %bitcast.7), calls=%async_computation.5 | async-start | bytes 8388608
  0.7 7.0 %slice-start.4 = ((s8[18874368]{0:T(1024)(128)(4,1)}), s8[2097152]{0:T(1024)(128)(4,1)S(1)}, s32[]{:S(2)}) async-start(s8[18874368]{0:T(1024)(128)(4,1)} %bitcast.7), calls=%async_computation.6 | async-start | bytes 4194304
  4.4 31.1 %copy-start.1 = (bf16[32,1,64,256]{3,2,1,0:T(8,128)(2,1)S(1)}, bf16[32,1,64,256]{3,2,1,0:T(8,128)(2,1)}, u32[]{:S(2)}) copy-start(bf16[32,1,64,256]{3,2,1,0:T(8,128)(2,1)} %param.12) | copy-start | bytes 3145732
  11.0 14.8 %all-to-all-start = ((f32[8,36,128]{2,1,0:T(8,128)}), f32[8,36,128]{2,1,0:T(8,128)S(1)}, u32[]{:S(2)}, u32[]{:S(2)}) async-start(f32[8,36,128]{2,1,0:T(8,128)} %bitcast.1), calls=%async_computation | async-start | bytes 327680 | tf_op jit(solution)/shard_map/all_to_all | solution.py:395
  18.2 23.4 %collective-permute-start = (bf16[9,64,256]{2,1,0:T(8,128)(2,1)}, bf16[9,64,256]{2,1,0:T(8,128)(2,1)}, u32[]{:S(2)}, u32[]{:S(2)}) collective-permute-start(bf16[9,64,256]{2,1,0:T(8,128)(2,1)} %get-tuple-element.11._after), channel_id=1, source_target_pairs={{0,8},{8,0},{16,24},{24,16},{1,9},{9,1},{17,25},{25,17},{2,10},{10... | collective-permute-start | bytes 884744 | tf_op jit(solution)/shard_map/ppermute | solution.py:392
  18.3 23.4 %collective-permute-start.1 = (bf16[9,64,256]{2,1,0:T(8,128)(2,1)}, bf16[9,64,256]{2,1,0:T(8,128)(2,1)}, u32[]{:S(2)}, u32[]{:S(2)}) collective-permute-start(bf16[9,64,256]{2,1,0:T(8,128)(2,1)} %get-tuple-element.14), channel_id=1, source_target_pairs={{0,16},{8,24},{16,0},{24,8},{1,17},{9,25},{17,1},{25,9},{2,18},{10... | collective-permute-start | bytes 884744 | tf_op jit(solution)/shard_map/ppermute | solution.py:392
  19.8 21.8 %collective-permute-start.2 = (bf16[9,64,256]{2,1,0:T(8,128)(2,1)}, bf16[9,64,256]{2,1,0:T(8,128)(2,1)}, u32[]{:S(2)}, u32[]{:S(2)}) collective-permute-start(bf16[9,64,256]{2,1,0:T(8,128)(2,1)} %get-tuple-element.15), channel_id=1, source_target_pairs={{0,24},{8,16},{16,8},{24,0},{1,25},{9,17},{17,9},{25,1},{2,26},{10... | collective-permute-start | bytes 884744 | tf_op jit(solution)/shard_map/ppermute | solution.py:392
  35.5 6.2 %copy-start = (bf16[2048,4096]{1,0:T(8,128)(2,1)S(1)}, bf16[2048,4096]{1,0:T(8,128)(2,1)}, u32[]{:S(2)}) copy-start(bf16[2048,4096]{1,0:T(8,128)(2,1)} %weight.3) | copy-start | bytes 50331652

commit v5 on v4

--- a/solution.py
+++ b/solution.py
@@ -181,45 +181,40 @@
 
 
 def project_body(tokens, weight, _after, out):
-    groups, heads, rows, head_dim = out.shape
-    parts = GRP + 2
-    reqs = rows // parts
+    groups, heads, reqs, width = out.shape
     depth = weight.shape[0]
     if tokens.shape[1] != depth:
         block = lax.axis_index("src") * lax.axis_size("dst") + lax.axis_index("dst")
         values = tokens[:, pl.ds(pl.multiple_of(block * depth, depth), depth)]
     else:
         values = tokens[...]
-    width = parts * head_dim
     for h in range(heads):
         result = jnp.dot(
             values, weight[:, h * width : (h + 1) * width], preferred_element_type=jnp.float32
         )
         for g in range(groups):
-            for part in range(parts):
-                out[g, h, part * reqs : (part + 1) * reqs, :] = result[
-                    g * reqs : (g + 1) * reqs, part * head_dim : (part + 1) * head_dim
-                ]
+            out[g, h] = result[g * reqs : (g + 1) * reqs]
 
 
 def project(tokens, weight, groups, after):
-    reqs = tokens.shape[0] // groups
-    parts = GRP + 2
-    head_dim = weight.shape[1] // (KVH * parts)
+    reqs, width = tokens.shape[0] // groups, weight.shape[1] // KVH
     return pl.pallas_call(
         project_body,
         in_specs=[VMEM, VMEM, ANY],
         out_specs=VMEM,
-        out_shape=jax.ShapeDtypeStruct((groups, KVH, parts * reqs, head_dim), jnp.float32),
+        out_shape=jax.ShapeDtypeStruct((groups, KVH, reqs, width), jnp.float32),
         compiler_params=pltpu.CompilerParams(vmem_limit_bytes=8 * 1024 * 1024),
         name="project",
     )(tokens, weight, after)
 
 
-def attend_body(parts, pool, live, turns, out):
-    total = functools.reduce(jnp.add, [parts[i] for i in range(parts.shape[0])])
-    head_dim = total.shape[1]
+def attend_body(shares, pool, live, turns, out, split):
+    head_dim = split.shape[1]
     reqs = live.shape[0]
+    joined = functools.reduce(jnp.add, [shares[i] for i in range(shares.shape[0])])
+    for part in range(GRP + 2):
+        split[part * reqs : (part + 1) * reqs] = joined[:, part * head_dim : (part + 1) * head_dim]
+    total = split[...]
     rows = GRP * reqs
 
     def per_row(values, count):
@@ -261,17 +256,18 @@
     out[:, head_dim:] = jnp.where(lane < head_dim // 2, top, total_weight)
 
 
-def attend(parts, pool, live, turns):
+def attend(shares, pool, live, turns):
     reqs = live.shape[0]
     return pl.pallas_call(
         attend_body,
         out_shape=jax.ShapeDtypeStruct((GRP * reqs, pool.shape[2]), jnp.float32),
         in_specs=[VMEM] * 4,
         out_specs=VMEM,
+        scratch_shapes=[pltpu.VMEM(((GRP + 2) * reqs, pool.shape[2] // 2), jnp.float32)],
         compiler_params=pltpu.CompilerParams(vmem_limit_bytes=16 * 1024 * 1024),
         cost_estimate=pl.CostEstimate(flops=10**12, bytes_accessed=2**26, transcendentals=0),
         name="attend",
-    )(parts, pool, live, turns)
+    )(shares, pool, live, turns)
 
 
 def merge(parts):

time: 59 us -> 58.9 us (level)
  no operation moved by 1% of the time
where the time goes in v5:
time: 58.9 us; the launch traced here: 58.7 us
  blocking collectives  28.5 us (48%)
  Pallas kernels  10.6 us (18%)
  starting transfers between devices  9.13 us (16%)
  waiting for transfers between devices  5.6 us (10%)
  local copies, waits for them, and re-layouts  3.31 us (6%)
  other arithmetic  0.78 us (1%)
  between operations  0.75 us (1%)
    all_to_all x1, blocking collectives, shards(): lax.all_to_all(outgoing, 'dst', split_axis=0, concat_axis=0, tiled=True)  13.3 us
    all_gather x1, blocking collectives, shards(): projected = lax.all_gather(jnp.sum(shares, axis=0), 'src')  9.67 us
    all_to_all x1, starting transfers between devices, shards(): lax.all_to_all(partial, 'dst', split_axis=0, concat_axis=0, tiled=True)  7.28 us
    all_to_all x1, waiting for transfers between devices, shards(): lax.all_to_all(partial, 'dst', split_axis=0, concat_axis=0, tiled=True)  5.59 us
    all_gather x1, blocking collectives, shards(): heads = lax.all_gather(mine, 'src')  5.54 us
    pallas_call x1, Pallas kernels, prepare(): pl.pallas_call(functools.partial(prepare_body, reqs), in_specs=[ANY] * 6,...  3.71 us
    unnamed x16, local copies, waits for them, and re-layouts  3.31 us
    pallas_call x1, Pallas kernels, project(): pl.pallas_call(project_body, in_specs=[VMEM, VMEM, ANY], out_specs=VMEM,...  3.23 us
  transfers between devices with their start and end apart: 4, of which 1 were waited for; matrix products, arithmetic and copies ran while one was open for 0% of the time, Pallas kernels for 1%

profile of v5, /device:TPU:0, one launch (start us, length us, event | category | flops | bytes accessed | tf_op | source)
XLA Modules:
  0.0 58.7 jit_solution(7876265755266427624)
XLA Ops:
  0.7 0.0 slice-start.1
  0.7 0.0 slice-start.2
  0.7 0.0 slice-start.4
  0.7 3.7 %prepare.1 = (bf16[9,64,256]{2,1,0:T(8,128)(2,1)}, bf16[9,64,256]{2,1,0:T(8,128)(2,1)}, bf16[9,64,256]{2,1,0:T(8,128)(2,1)}, f32[2,2048]{1,0:T(2,128)S(1)}, f32[2,2,128]{2,1,0:T(2,128)S(1)}, /*index=5*/s32[41]{0:T(128)S(1)}) custom-call(s32[1,128]{1,0:T(1,128)} %handoff_in.1, s32[2,96]{1,0:T(2,128)} %table_in.1, s32[2]{0:T(128)} %lengths_in.1, ...), custom_call_target="tpu_custom_call" | custom-call | flops 10000000000 | bytes 33554432 | tf_op jit(solution)/shard_map/prepare/pallas_call | solution.py:157
  4.4 0.0 copy-start.1
  4.4 0.3 slice-done.1
  4.7 1.2 %slice-done.2 = s8[4194304]{0:T(1024)(128)(4,1)S(1)} async-done(((s8[18874368]{0:T(1024)(128)(4,1)}), s8[4194304]{0:T(1024)(128)(4,1)S(1)}, s32[]{:S(2)}) %slice-start.2) | async-done | bytes 4194328
  5.9 1.2 %slice-done.3 = s8[4194304]{0:T(1024)(128)(4,1)S(1)} async-done(((s8[18874368]{0:T(1024)(128)(4,1)}), s8[4194304]{0:T(1024)(128)(4,1)S(1)}, s32[]{:S(2)}) %slice-start.3) | async-done | bytes 4194328
  7.1 0.6 %slice-done.4 = s8[2097152]{0:T(1024)(128)(4,1)S(1)} async-done(((s8[18874368]{0:T(1024)(128)(4,1)}), s8[2097152]{0:T(1024)(128)(4,1)S(1)}, s32[]{:S(2)}) %slice-start.4) | async-done | bytes 2097176
  7.7 3.2 %project.1 = f32[1,8,2,2304]{3,2,1,0:T(2,128)} custom-call(bf16[2,16384]{1,0:T(2,128)(2,1)S(1)} %copy-done.2, bf16[512,18432]{1,0:T(8,128)(2,1)S(1)} %bitcast.8, bf16[9,64,256]{2,1,0:T(8,128)(2,1)} %get-tuple-element.11._after), custom_call_target="tpu_custom_call" | custom-call | tf_op jit(solution)/shard_map/project/pallas_call | solution.py:201
  11.0 7.3 %all-to-all-start = ((f32[8,2,2304]{2,1,0:T(2,128)}), f32[8,2,2304]{2,1,0:T(2,128)S(1)}, u32[]{:S(2)}, u32[]{:S(2)}) async-start(f32[8,2,2304]{2,1,0:T(2,128)} %bitcast.1), calls=%async_computation | async-start | bytes 294912 | tf_op jit(solution)/shard_map/all_to_all | solution.py:391
  18.2 0.0 collective-permute-start
  18.2 1.6 %collective-permute-start.1 = (bf16[9,64,256]{2,1,0:T(8,128)(2,1)}, bf16[9,64,256]{2,1,0:T(8,128)(2,1)}, u32[]{:S(2)}, u32[]{:S(2)}) collective-permute-start(bf16[9,64,256]{2,1,0:T(8,128)(2,1)} %get-tuple-element.14), channel_id=1, source_target_pairs={{0,16},{8,24},{16,0},{24,8},{1,17},{9,25},{17,1},{25,9},{2,18},{10... | collective-permute-start | bytes 884744 | tf_op jit(solution)/shard_map/ppermute | solution.py:388
  19.8 0.3 collective-permute-start.2
  20.1 5.6 %all-to-all-done = f32[8,2,2304]{2,1,0:T(2,128)S(1)} async-done(((f32[8,2,2304]{2,1,0:T(2,128)}), f32[8,2,2304]{2,1,0:T(2,128)S(1)}, u32[]{:S(2)}, u32[]{:S(2)}) %all-to-all-start) | async-done | bytes 147488 | tf_op jit(solution)/shard_map/all_to_all | solution.py:391
  25.7 0.1 reduce_sum.18
  25.7 9.7 %all-gather.2.shares = f32[4,2,2304]{2,1,0:T(2,128)S(1)} all-gather(f32[1,2,2304]{2,1,0:T(2,128)S(1)} %bitcast.13), channel_id=2, replica_groups=mesh['src'=4,'dst'=8] {'src'}, dimensions={0}, use_global_device_ids=true | all-gather | bytes 92160 | tf_op jit(solution)/shard_map/all_gather | solution.py:392
  35.4 0.6 %attend.1 = f32[32,256]{1,0:T(8,128)S(1)} custom-call(f32[4,2,2304]{2,1,0:T(2,128)S(1)} %all-gather.2.shares, bf16[32,64,256]{2,1,0:T(8,128)(2,1)S(1)} %bitcast.10, f32[2,2048]{1,0:T(2,128)S(1)} %get-tuple-element.12.live, f32[2,2,128]{2,1,0:T(2,128)S(1)} %get-tuple-element.13.turns), custom_call_target="tpu_custom_call" | custom-call | flops 999999995904 | bytes 67108864 | tf_op jit(solution)/shard_map/attend/pallas_call | solution.py:261
  36.0 5.5 %all-gather.1 = f32[128,256]{1,0:T(8,128)S(1)} all-gather(f32[32,256]{1,0:T(8,128)S(1)} %attend.1), channel_id=3, replica_groups=mesh['src'=4,'dst'=8] {'src'}, dimensions={0}, use_global_device_ids=true | all-gather | bytes 163840 | tf_op jit(solution)/shard_map/all_gather | solution.py:394
  41.6 0.0 collective-permute-done.1.rest_1_
  41.6 0.0 collective-permute-done.2.rest_2_
  41.6 3.0 %output.1 = (bf16[8,2,4096]{2,1,0:T(2,128)(2,1)S(1)}, bf16[32,64,256]{2,1,0:T(8,128)(2,1)}) custom-call(s32[41]{0:T(128)S(1)} %get-tuple-element.10.source_in, f32[4,32,256]{2,1,0:T(8,128)S(1)} %bitcast.12, bf16[2048,4096]{1,0:T(8,128)(2,1)S(1)} %copy-done, bf16[32,64,256]{2,1,0:T(8,128)(2,1)S(1)} %bitcast.11, ...), custom_call_target="tpu_custom_call" | custom-call | tf_op jit(solution)/shard_map/output/pallas_call | solution.py:349
  44.6 13.3 %all_to_all.10 = bf16[8,2,4096]{2,1,0:T(2,128)(2,1)S(1)} all-to-all(bf16[8,2,4096]{2,1,0:T(2,128)(2,1)S(1)} %get-tuple-element.16), channel_id=1, replica_groups=mesh['src'=4,'dst'=8] {'dst'}, dimensions={0} | all-to-all | bytes 262144 | tf_op jit(solution)/shard_map/all_to_all | solution.py:410
  57.9 0.7 %convert_reduce_fusion = f32[2,4096]{1,0:T(2,128)} fusion(bf16[8,2,4096]{2,1,0:T(2,128)(2,1)S(1)} %all_to_all.10), kind=kLoop, calls=%fused_computation | loop fusion | flops 122880 | bytes 163840 | tf_op jit(solution)/shard_map/reduce_sum | solution.py:411
  (10 shorter events, 0.0 us)
Async XLA Ops:
  0.6 3.8 %slice-start = ((s8[18874368]{0:T(1024)(128)(4,1)}), s8[4194304]{0:T(1024)(128)(4,1)S(1)}, s32[]{:S(2)}) async-start(s8[18874368]{0:T(1024)(128)(4,1)} %bitcast.7), calls=%async_computation.2 | async-start | bytes 8388608
  0.6 3.8 %copy-start.2 = (bf16[2,16384]{1,0:T(2,128)(2,1)S(1)}, bf16[2,16384]{1,0:T(2,128)(2,1)}, u32[]{:S(2)}) copy-start(bf16[2,16384]{1,0:T(2,128)(2,1)} %tokens.1) | copy-start | bytes 196612
  0.7 4.1 %slice-start.1 = ((s8[18874368]{0:T(1024)(128)(4,1)}), s8[4194304]{0:T(1024)(128)(4,1)S(1)}, s32[]{:S(2)}) async-start(s8[18874368]{0:T(1024)(128)(4,1)} %bitcast.7), calls=%async_computation.3 | async-start | bytes 8388608
  0.7 5.3 %slice-start.2 = ((s8[18874368]{0:T(1024)(128)(4,1)}), s8[4194304]{0:T(1024)(128)(4,1)S(1)}, s32[]{:S(2)}) async-start(s8[18874368]{0:T(1024)(128)(4,1)} %bitcast.7), calls=%async_computation.4 | async-start | bytes 8388608
  0.7 6.5 %slice-start.3 = ((s8[18874368]{0:T(1024)(128)(4,1)}), s8[4194304]{0:T(1024)(128)(4,1)S(1)}, s32[]{:S(2)}) async-start(s8[18874368]{0:T(1024)(128)(4,1)} %bitcast.7), calls=%async_computation.5 | async-start | bytes 8388608
  0.7 7.0 %slice-start.4 = ((s8[18874368]{0:T(1024)(128)(4,1)}), s8[2097152]{0:T(1024)(128)(4,1)S(1)}, s32[]{:S(2)}) async-start(s8[18874368]{0:T(1024)(128)(4,1)} %bitcast.7), calls=%async_computation.6 | async-start | bytes 4194304
  4.4 31.0 %copy-start.1 = (bf16[32,1,64,256]{3,2,1,0:T(8,128)(2,1)S(1)}, bf16[32,1,64,256]{3,2,1,0:T(8,128)(2,1)}, u32[]{:S(2)}) copy-start(bf16[32,1,64,256]{3,2,1,0:T(8,128)(2,1)} %param.12) | copy-start | bytes 3145732
  11.0 14.7 %all-to-all-start = ((f32[8,2,2304]{2,1,0:T(2,128)}), f32[8,2,2304]{2,1,0:T(2,128)S(1)}, u32[]{:S(2)}, u32[]{:S(2)}) async-start(f32[8,2,2304]{2,1,0:T(2,128)} %bitcast.1), calls=%async_computation | async-start | bytes 294912 | tf_op jit(solution)/shard_map/all_to_all | solution.py:391
  18.2 23.3 %collective-permute-start = (bf16[9,64,256]{2,1,0:T(8,128)(2,1)}, bf16[9,64,256]{2,1,0:T(8,128)(2,1)}, u32[]{:S(2)}, u32[]{:S(2)}) collective-permute-start(bf16[9,64,256]{2,1,0:T(8,128)(2,1)} %get-tuple-element.11._after), channel_id=1, source_target_pairs={{0,8},{8,0},{16,24},{24,16},{1,9},{9,1},{17,25},{25,17},{2,10},{10... | collective-permute-start | bytes 884744 | tf_op jit(solution)/shard_map/ppermute | solution.py:388
  18.2 23.3 %collective-permute-start.1 = (bf16[9,64,256]{2,1,0:T(8,128)(2,1)}, bf16[9,64,256]{2,1,0:T(8,128)(2,1)}, u32[]{:S(2)}, u32[]{:S(2)}) collective-permute-start(bf16[9,64,256]{2,1,0:T(8,128)(2,1)} %get-tuple-element.14), channel_id=1, source_target_pairs={{0,16},{8,24},{16,0},{24,8},{1,17},{9,25},{17,1},{25,9},{2,18},{10... | collective-permute-start | bytes 884744 | tf_op jit(solution)/shard_map/ppermute | solution.py:388
  19.8 21.8 %collective-permute-start.2 = (bf16[9,64,256]{2,1,0:T(8,128)(2,1)}, bf16[9,64,256]{2,1,0:T(8,128)(2,1)}, u32[]{:S(2)}, u32[]{:S(2)}) collective-permute-start(bf16[9,64,256]{2,1,0:T(8,128)(2,1)} %get-tuple-element.15), channel_id=1, source_target_pairs={{0,24},{8,16},{16,8},{24,0},{1,25},{9,17},{17,9},{25,1},{2,26},{10... | collective-permute-start | bytes 884744 | tf_op jit(solution)/shard_map/ppermute | solution.py:388
  35.4 6.2 %copy-start = (bf16[2048,4096]{1,0:T(8,128)(2,1)S(1)}, bf16[2048,4096]{1,0:T(8,128)(2,1)}, u32[]{:S(2)}) copy-start(bf16[2048,4096]{1,0:T(8,128)(2,1)} %weight.3) | copy-start | bytes 50331652
